TPU v7x, 128 devices: a whole 4x4x4 slice. The times are simulated.
128 devices in a mesh: dp: 1, tp: 2 (over core), ep: 64 (over z, y, x).
Axes of the slice: x: 4, y: 4, z: 4, core: 2. Of those that a mesh axis runs over, the one named last changes fastest.
Arguments:
- hidden_in: bfloat16 [2048, 2048], P(('dp', 'ep'))
- positions: int32 [2048], P(('dp', 'ep'))
- expert_ids: int32 [2048, 2], P(('dp', 'ep'))
- k_cache: bfloat16 [2048, 32, 4, 128], P(('dp', 'ep'), None, 'tp')
- v_cache: bfloat16 [2048, 32, 4, 128], P(('dp', 'ep'), None, 'tp')
- norm_in: bfloat16 [2048], replicated
- norm_res: bfloat16 [2048], replicated
- norm_post: bfloat16 [2048], replicated
- w_q: bfloat16 [2048, 4096], P(None, 'tp')
- w_k: bfloat16 [2048, 512], P(None, 'tp')
- w_v: bfloat16 [2048, 512], P(None, 'tp')
- w_o: bfloat16 [4096, 2048], P('tp')
- w_gate: bfloat16 [2048, 6144], P(None, 'tp')
- w_up: bfloat16 [2048, 6144], P(None, 'tp')
- w_down: bfloat16 [6144, 2048], P('tp')
- w_router: bfloat16 [2048, 128], replicated
- e_gate: bfloat16 [128, 2048, 768], P('ep', None, 'tp')
- e_up: bfloat16 [128, 2048, 768], P('ep', None, 'tp')
- e_down: bfloat16 [128, 768, 2048], P('ep', 'tp')
Outputs:
- output 1: bfloat16 [2048, 2048], P(('dp', 'ep'))
- output 2: bfloat16 [2048, 32, 4, 128], P(('dp', 'ep'), None, 'tp')
- output 3: bfloat16 [2048, 32, 4, 128], P(('dp', 'ep'), None, 'tp')
All inputs are finite; a program needn't handle non-finite values.
Results may differ from a plain program's by a relative error of at most 0.0124179.
Values are sent between devices in bfloat16 or wider.
A program may use at most 1 GiB of HBM per device.

v0:
```python
import jax
import jax.numpy as jnp
from jax import lax
from jax.sharding import PartitionSpec as P

NORM_EPS = 1e-5
ROPE_BASE = 10000.0


def rms_norm(values, gain_vec):
    wide_vals = values.astype(jnp.float32)
    inv_rms = lax.rsqrt(jnp.mean(wide_vals * wide_vals, axis=-1, keepdims=True) + NORM_EPS)
    return (wide_vals * inv_rms * gain_vec.astype(jnp.float32)).astype(jnp.bfloat16)


def rope_rotate(values, positions):
    half_dim = values.shape[-1] // 2
    inv_freq = 1.0 / (ROPE_BASE ** (jnp.arange(0, 2 * half_dim, 2, dtype=jnp.float32) / (2 * half_dim)))
    angles = positions.astype(jnp.float32)[:, None] * inv_freq[None, :]
    cosine = jnp.cos(angles)[:, None, :]
    sine_part = jnp.sin(angles)[:, None, :]
    first_half = values[..., :half_dim]
    second_half = values[..., half_dim:]
    return jnp.concatenate([first_half * cosine - second_half * sine_part, second_half * cosine + first_half * sine_part], axis=-1)


def attention_block(normed, positions, k_cache, v_cache, w_q, w_k, w_v):
    tokens = normed.shape[0]
    cache_len, kv_heads, head_dim = k_cache.shape[1], k_cache.shape[2], k_cache.shape[3]
    q_heads = w_q.shape[1] // head_dim
    group_size = q_heads // kv_heads
    q_proj = jnp.dot(normed, w_q, preferred_element_type=jnp.float32).reshape(tokens, q_heads, head_dim)
    k_proj = jnp.dot(normed, w_k, preferred_element_type=jnp.float32).reshape(tokens, kv_heads, head_dim)
    v_new = jnp.dot(normed, w_v, preferred_element_type=jnp.float32).astype(jnp.bfloat16).reshape(tokens, kv_heads, head_dim)
    q_rot = rope_rotate(q_proj, positions).astype(jnp.bfloat16).reshape(tokens, kv_heads, group_size, head_dim)
    k_rot = rope_rotate(k_proj, positions).astype(jnp.bfloat16)
    slot_hit = (jnp.arange(cache_len)[None, :] == positions[:, None])[:, :, None, None]
    k_out = jnp.where(slot_hit, k_rot[:, None], k_cache)
    v_out = jnp.where(slot_hit, v_new[:, None], v_cache)
    scores = jnp.einsum('bkgd,btkd->bkgt', q_rot, k_out, preferred_element_type=jnp.float32) * (head_dim ** -0.5)
    visible = jnp.arange(cache_len)[None, None, None, :] <= positions[:, None, None, None]
    attn_probs = jax.nn.softmax(jnp.where(visible, scores, -jnp.inf), axis=-1).astype(jnp.bfloat16)
    mixed_vals = jnp.einsum('bkgt,btkd->bkgd', attn_probs, v_out, preferred_element_type=jnp.float32)
    return mixed_vals.astype(jnp.bfloat16).reshape(tokens, q_heads * head_dim), k_out, v_out


def dense_block(hidden_mid, norm_res, w_gate, w_up, w_down):
    res_in = rms_norm(hidden_mid, norm_res)
    gate_val = jnp.dot(res_in, w_gate, preferred_element_type=jnp.float32)
    up_val = jnp.dot(res_in, w_up, preferred_element_type=jnp.float32)
    act_val = (jax.nn.silu(gate_val) * up_val).astype(jnp.bfloat16)
    return jnp.dot(act_val, w_down, preferred_element_type=jnp.float32)


def route_weights(moe_in, w_router, expert_ids):
    gate_probs = jax.nn.softmax(jnp.dot(moe_in, w_router, preferred_element_type=jnp.float32), axis=-1)
    picked = jnp.take_along_axis(gate_probs, expert_ids, axis=1)
    return picked / jnp.sum(picked, axis=1, keepdims=True)


def run_experts(slot_rows, slot_expert, e_gate, e_up, e_down):
    sort_order = jnp.argsort(slot_expert, stable=True)
    sorted_rows = slot_rows[sort_order]
    group_sizes = jnp.bincount(slot_expert, length=e_gate.shape[0]).astype(jnp.int32)
    gate_val = lax.ragged_dot(sorted_rows, e_gate, group_sizes, preferred_element_type=jnp.float32)
    up_val = lax.ragged_dot(sorted_rows, e_up, group_sizes, preferred_element_type=jnp.float32)
    act_val = (jax.nn.silu(gate_val) * up_val).astype(jnp.bfloat16)
    out_sorted = lax.ragged_dot(act_val, e_down, group_sizes, preferred_element_type=jnp.float32).astype(jnp.bfloat16)
    return out_sorted[jnp.argsort(sort_order)]


def solution(mesh):
    ep_size = mesh.shape['ep']
    row_spec = P(('dp', 'ep'), None)
    cache_spec = P(('dp', 'ep'), None, 'tp', None)
    col_split = P(None, 'tp')
    row_split = P('tp', None)
    in_specs = (row_spec, P(('dp', 'ep')), row_spec, cache_spec, cache_spec, P(None), P(None), P(None), col_split, col_split, col_split, row_split, col_split, col_split, row_split, P(None, None), P('ep', None, 'tp'), P('ep', None, 'tp'), P('ep', 'tp', None))
    out_specs = (row_spec, cache_spec, cache_spec)

    def local_layer(hidden_in, positions, expert_ids, k_cache, v_cache, norm_in, norm_res, norm_post, w_q, w_k, w_v, w_o, w_gate, w_up, w_down, w_router, e_gate, e_up, e_down):
        tokens, model_dim = hidden_in.shape
        local_experts = e_gate.shape[0]
        capacity = 4 * tokens // ep_size
        attn_mix, k_out, v_out = attention_block(rms_norm(hidden_in, norm_in), positions, k_cache, v_cache, w_q, w_k, w_v)
        attn_sum = lax.psum(jnp.dot(attn_mix, w_o, preferred_element_type=jnp.float32).astype(jnp.bfloat16), 'tp')
        hidden_mid = (hidden_in.astype(jnp.float32) + attn_sum.astype(jnp.float32)).astype(jnp.bfloat16)
        dense_sum = lax.psum(dense_block(hidden_mid, norm_res, w_gate, w_up, w_down).astype(jnp.bfloat16), 'tp')
        moe_in = rms_norm(hidden_in, norm_post)
        route_wts = route_weights(moe_in, w_router, expert_ids)
        flat_ids = expert_ids.reshape(-1)
        dest_shard = flat_ids // local_experts
        dest_hot = (dest_shard[:, None] == jnp.arange(ep_size)[None, :]).astype(jnp.int32)
        rank_in_dest = jnp.sum((jnp.cumsum(dest_hot, axis=0) - dest_hot) * dest_hot, axis=1)
        slot_index = dest_shard * capacity + rank_in_dest
        pair_token = jnp.arange(2 * tokens, dtype=jnp.int32) // 2
        send_token = jnp.full((ep_size * capacity,), tokens, jnp.int32).at[slot_index].set(pair_token)
        send_expert = jnp.zeros((ep_size * capacity,), jnp.int32).at[slot_index].set(flat_ids % local_experts)
        padded_rows = jnp.concatenate([moe_in, jnp.zeros((1, model_dim), jnp.bfloat16)], axis=0)
        send_rows = padded_rows[send_token]
        recv_rows = lax.all_to_all(send_rows, 'ep', 0, 0, tiled=True)
        recv_expert = lax.all_to_all(send_expert, 'ep', 0, 0, tiled=True)
        expert_part = run_experts(recv_rows, recv_expert, e_gate, e_up, e_down)
        expert_sum = lax.psum(expert_part, 'tp')
        returned = lax.all_to_all(expert_sum, 'ep', 0, 0, tiled=True)
        pair_out = returned[slot_index].reshape(tokens, 2, model_dim)
        moe_out = jnp.sum(route_wts[:, :, None] * pair_out, axis=1)
        hidden_out = (hidden_mid.astype(jnp.float32) + dense_sum.astype(jnp.float32) + moe_out).astype(jnp.bfloat16)
        return hidden_out, k_out, v_out

    return jax.shard_map(local_layer, mesh=mesh, in_specs=in_specs, out_specs=out_specs, check_vma=False)
```

profile of v0, /device:TPU:1, one launch (start us, length us, event | category | flops | bytes accessed | tf_op | source)
XLA Modules:
  0.0 183.0 jit_solution(16272957447342756161)
XLA Ops:
  7.2 0.9 copy.61
  8.7 0.8 scatter_custom_fusion.1
  9.5 0.7 all_to_all.27
  10.2 12.0 %all-to-all-start.1 = ((s32[64,2,1]{1,2,0:T(1,128)}), s32[64,2,1]{1,2,0:T(1,128)S(1)}, u32[]{:S(2)}, u32[]{:S(2)}) async-start(s32[64,2,1]{1,2,0:T(1,128)} %bitcast.5), calls=%async_computation.1 | async-start | bytes 65536 | tf_op jit(solution)/shard_map/all_to_all | solution.py:102
  22.3 0.7 iota_compare_fusion.2
  23.0 0.7 convert_element_type.86
  23.7 0.7 convert_element_type.84
  24.3 1.0 fusion.16
  25.4 1.2 fusion.49
  26.7 1.6 convolution_convert_fusion.3
  28.3 5.1 %convolution_bitcast_fusion = f32[4,8,16,128]{3,1,2,0:T(8,128)S(1)} fusion(bf16[2048,2048]{1,0:T(8,128)(2,1)} %param.27, bf16[32,2048]{1,0:T(8,128)(2,1)} %param.19, f32[2048]{0:T(1024)S(1)} %convert_element_type.84, f32[32]{0:T(128)S(1)} %add_rsqrt_fusion.1), kind=kOutput, calls=%fused_computation.15 | convolution fusion | flops 268697600 | bytes 8790144 | tf_op jit(solution)/shard_map/dot_general | solution.py:32
  34.0 1.5 broadcast_select_fusion.1
  35.5 0.4 fusion.3
  36.0 0.3 fusion.55
  36.3 1.0 convolution_convert_fusion.2
  37.3 5.6 %convolution_convert_fusion.1 = bf16[32,2048]{1,0:T(8,128)(2,1)} fusion(bf16[2048,2048]{1,0:T(8,128)(2,1)} %param.30, bf16[4,8,16,128]{3,2,1,0:T(8,128)(2,1)S(1)} %bitcast.36), kind=kOutput, calls=%fused_computation.12 | convolution fusion | flops 268500992 | bytes 8650752 | tf_op jit(solution)/shard_map/dot_general | solution.py:86
  42.9 0.8 scatter_custom_fusion
  43.7 0.5 broadcast.352
  44.2 0.7 fusion.52
  45.1 2.5 %sort.34 = (s32[128]{0:T(128)}, s32[128]{0:T(128)S(1)}) sort(s32[128]{0:T(128)S(1)} %all_to_all.29, s32[128]{0:T(128)S(1)} %iota.38), dimensions={0}, to_apply=%region_13.14 | sort | flops 896 | bytes 2048 | tf_op jit(solution)/shard_map/jit(argsort)/sort | solution.py:62
  47.7 2.5 %sort.35 = (s32[128]{0:T(128)}, s32[128]{0:T(128)S(1)}) sort(s32[128]{0:T(128)S(1)} %get-tuple-element.5, s32[128]{0:T(128)S(1)} %iota.39), dimensions={0}, to_apply=%region_15.16 | sort | flops 896 | bytes 2048 | tf_op jit(solution)/shard_map/jit(argsort)/sort | solution.py:69
  50.4 1.9 %scatter_custom_fusion.2 = s32[2]{0:T(128)} fusion(s32[128]{0:T(128)S(1)} %reshape.359, s32[128]{0:T(128)S(1)} %broadcast.286, s32[]{:T(128)} %constant.87.clone.1), kind=kCustom, calls=%fused_computation.105 | custom fusion | flops 128 | bytes 12 | tf_op jit(solution)/shard_map/scatter-add | solution.py:64
  52.3 1.3 ragged-dot-metadata
  53.6 14.8 %all-reduce.5.cloned.1.call-done = bf16[32,2048]{1,0:T(8,128)(2,1)} async-done(((bf16[32,2048]{1,0:T(8,128)(2,1)}), bf16[32,2048]{1,0:T(8,128)(2,1)}) %all-reduce.5.cloned.1.call-update) | async-done | bytes 131088 | tf_op jit(solution)/shard_map/psum | solution.py:86
  68.4 1.1 fusion.18
  69.5 0.9 gather_fusion
  70.5 1.1 all_to_all.24
  71.6 10.1 %all-to-all-start = ((bf16[64,2,2048]{2,1,0:T(2,128)(2,1)}), bf16[64,2,2048]{2,1,0:T(2,128)(2,1)S(1)}, u32[]{:S(2)}, u32[]{:S(2)}) async-start(bf16[64,2,2048]{2,1,0:T(2,128)(2,1)} %all_to_all.24), calls=%async_computation | async-start | bytes 1048576 | tf_op jit(solution)/shard_map/all_to_all | solution.py:101
  81.7 0.2 all-reduce.7.cloned.1.call-start
  82.0 6.9 %fusion.34 = f32[32,3072]{1,0:T(8,128)S(1)} fusion(bf16[2048,3072]{1,0:T(8,128)(2,1)} %param.31, bf16[32,2048]{1,0:T(8,128)(2,1)S(1)} %get-tuple-element.26, f32[2048]{0:T(1024)S(1)} %convert_element_type.94, f32[32]{0:T(128)S(1)} %add_rsqrt_fusion), kind=kOutput, calls=%fused_computation.60 | convolution fusion | flops 402915328 | bytes 13115520 | tf_op jit(solution)/shard_map/dot_general | solution.py:49
  88.9 13.3 %convolution_convert_fusion = bf16[32,2048]{1,0:T(8,128)(2,1)} fusion(bf16[3072,2048]{1,0:T(8,128)(2,1)} %param.33, bf16[2048,3072]{1,0:T(8,128)(2,1)} %param.32, f32[32,3072]{1,0:T(8,128)S(1)} %fusion.34, bf16[32,2048]{1,0:T(8,128)(2,1)S(1)} %get-tuple-element.26, f32[2048]{0:T(1024)S(1)} %convert_element_type.94, f32[32]{0:T(128)S(1)} %add_rsqrt_fusion), kind=kOutput, calls=%fused_computation.11 | convolution fusion | flops 806223872 | bytes 25829504 | tf_op jit(solution)/shard_map/dot_general | solution.py:52
  102.4 1.7 gather_fusion.1
  104.2 5.1 %ragged-dot-none.1 = f32[128,384]{1,0:T(8,128)} custom-call(s32[1]{0:T(128)} %get-tuple-element.7, s32[3]{0:T(128)} %get-tuple-element.8, s32[2]{0:T(128)} %get-tuple-element.9, s32[2]{0:T(128)} %get-tuple-element.10, s32[1]{0:T(128)} %get-tuple-element.7, bf16[128,2048]{1,0:T(8,128)(2,1)} %gather_fusion.1, bf16[2,2048,384]{2,1,0:T(8,128)(2,1)} %param.36), custom_call_target="tpu_custom_call" | custom-call | flops 201326592 | bytes 3866632 | tf_op jit(solution)/shard_map/ragged_dot_general/ragged-dot-none
  109.3 5.1 %ragged-dot-none.2 = f32[128,384]{1,0:T(8,128)} custom-call(s32[1]{0:T(128)} %get-tuple-element.7, s32[3]{0:T(128)} %get-tuple-element.8, s32[2]{0:T(128)} %get-tuple-element.9, s32[2]{0:T(128)} %get-tuple-element.10, s32[1]{0:T(128)} %get-tuple-element.7, bf16[128,2048]{1,0:T(8,128)(2,1)} %gather_fusion.1, bf16[2,2048,384]{2,1,0:T(8,128)(2,1)} %param.35), custom_call_target="tpu_custom_call" | custom-call | flops 201326592 | bytes 3866632 | tf_op jit(solution)/shard_map/ragged_dot_general/ragged-dot-none
  114.4 1.7 multiply_convert_fusion
  116.1 5.3 %ragged-dot-none = f32[128,2048]{1,0:T(8,128)} custom-call(s32[1]{0:T(128)} %get-tuple-element.7, s32[3]{0:T(128)} %get-tuple-element.8, s32[2]{0:T(128)} %get-tuple-element.9, s32[2]{0:T(128)} %get-tuple-element.10, s32[1]{0:T(128)} %get-tuple-element.7, bf16[128,384]{1,0:T(8,128)(2,1)} %multiply_convert_fusion, bf16[2,384,2048]{2,1,0:T(8,128)(2,1)} %param.37), custom_call_target="tpu_custom_call" | custom-call | flops 201326592 | bytes 4292616 | tf_op jit(solution)/shard_map/ragged_dot_general/ragged-dot-none
  121.4 1.3 convert_element_type.103
  122.7 0.9 gather_fusion.2
  123.7 1.2 all_to_all.30
  125.1 0.3 fusion.56
  125.6 25.2 %all-reduce.7.cloned.1.call-done = (bf16[64,2,2048]{2,1,0:T(2,128)(2,1)}, bf16[32,2048]{1,0:T(8,128)(2,1)}) async-done(((bf16[64,2,2048]{2,1,0:T(2,128)(2,1)}, bf16[32,2048]{1,0:T(8,128)(2,1)}), (bf16[64,2,2048]{2,1,0:T(2,128)(2,1)}, bf16[32,2048]{1,0:T(8,128)(2,1)})) %all-reduce.7.cloned.1.call-update) | async-done | bytes 655376 | tf_op jit(solution)/shard_map/psum | solution.py:104
  150.8 10.3 %all-to-all-start.2 = ((bf16[64,2,2048]{2,1,0:T(2,128)(2,1)}), bf16[64,2,2048]{2,1,0:T(2,128)(2,1)S(1)}, u32[]{:S(2)}, u32[]{:S(2)}) async-start(bf16[64,2,2048]{2,1,0:T(2,128)(2,1)} %get-tuple-element.21), calls=%async_computation.2 | async-start | bytes 1048576 | tf_op jit(solution)/shard_map/all_to_all | solution.py:105
  161.2 0.8 gather_fusion.4
  162.3 11.2 %all-to-all-done.2 = bf16[64,2,2048]{2,1,0:T(2,128)(2,1)S(1)} async-done(((bf16[64,2,2048]{2,1,0:T(2,128)(2,1)}), bf16[64,2,2048]{2,1,0:T(2,128)(2,1)S(1)}, u32[]{:S(2)}, u32[]{:S(2)}) %all-to-all-start.2) | async-done | bytes 524320 | tf_op jit(solution)/shard_map/all_to_all | solution.py:105
  173.6 0.7 gather_fusion.3
  174.4 0.3 reshape.302
  174.7 0.7 multiply_reduce_fusion
  175.5 0.7 fusion.22
  (74 shorter events, 2.9 us)
Async XLA Ops:
  7.2 18.2 %copy-start = (bf16[2048,256]{1,0:T(8,128)(2,1)S(1)}, bf16[2048,256]{1,0:T(8,128)(2,1)}, u32[]{:S(2)}) copy-start(bf16[2048,256]{1,0:T(8,128)(2,1)} %param.28) | copy-start | bytes 3145732
  7.2 26.8 %copy-start.5 = (bf16[32,32,2,128]{3,2,1,0:T(2,128)(2,1)S(1)}, bf16[32,32,2,128]{3,2,1,0:T(2,128)(2,1)}, u32[]{:S(2)}) copy-start(bf16[32,32,2,128]{3,2,1,0:T(2,128)(2,1)} %param.22) | copy-start | bytes 1572868
  7.2 26.8 %copy-start.6 = (bf16[32,32,2,128]{3,2,1,0:T(2,128)(2,1)S(1)}, bf16[32,32,2,128]{3,2,1,0:T(2,128)(2,1)}, u32[]{:S(2)}) copy-start(bf16[32,32,2,128]{3,2,1,0:T(2,128)(2,1)} %param.23) | copy-start | bytes 1572868
  10.2 33.5 %all-to-all-start.1 = ((s32[64,2,1]{1,2,0:T(1,128)}), s32[64,2,1]{1,2,0:T(1,128)S(1)}, u32[]{:S(2)}, u32[]{:S(2)}) async-start(s32[64,2,1]{1,2,0:T(1,128)} %bitcast.5), calls=%async_computation.1 | async-start | bytes 65536 | tf_op jit(solution)/shard_map/all_to_all | solution.py:102
  22.2 46.2 %all-reduce.5.cloned.1.call-start = ((), (), s32[]{:S(2)}) async-start(), calls=%async_computation.3 | async-start | bytes 262144 | tf_op jit(solution)/shard_map/psum | solution.py:86
  33.4 10.3 %copy-start.10 = (bf16[2048]{0:T(1024)(128)(2,1)S(1)}, bf16[2048]{0:T(1024)(128)(2,1)}, u32[]{:S(2)}) copy-start(bf16[2048]{0:T(1024)(128)(2,1)} %param.26) | copy-start | bytes 12292
  33.4 10.3 %copy-start.11 = (bf16[2048]{0:T(1024)(128)(2,1)S(1)}, bf16[2048]{0:T(1024)(128)(2,1)}, u32[]{:S(2)}) copy-start(bf16[2048]{0:T(1024)(128)(2,1)} %param.25) | copy-start | bytes 12292
  33.4 35.0 %copy-start.2 = (bf16[32,2048]{1,0:T(8,128)(2,1)S(1)}, bf16[32,2048]{1,0:T(8,128)(2,1)}, u32[]{:S(2)}) copy-start(bf16[32,2048]{1,0:T(8,128)(2,1)} %param.19) | copy-start | bytes 393220
  35.5 34.9 %copy-start.3 = (bf16[32,32,2,128]{3,2,1,0:T(2,128)(2,1)}, bf16[32,32,2,128]{3,2,1,0:T(2,128)(2,1)S(1)}, u32[]{:S(2)}) copy-start(bf16[32,32,2,128]{3,2,1,0:T(2,128)(2,1)S(1)} %get-tuple-element.32) | copy-start | bytes 1572868
  35.5 34.9 %copy-start.7 = (bf16[32,32,2,128]{3,2,1,0:T(2,128)(2,1)}, bf16[32,32,2,128]{3,2,1,0:T(2,128)(2,1)S(1)}, u32[]{:S(2)}) copy-start(bf16[32,32,2,128]{3,2,1,0:T(2,128)(2,1)S(1)} %get-tuple-element.33) | copy-start | bytes 1572868
  71.6 30.6 %all-to-all-start = ((bf16[64,2,2048]{2,1,0:T(2,128)(2,1)}), bf16[64,2,2048]{2,1,0:T(2,128)(2,1)S(1)}, u32[]{:S(2)}, u32[]{:S(2)}) async-start(bf16[64,2,2048]{2,1,0:T(2,128)(2,1)} %all_to_all.24), calls=%async_computation | async-start | bytes 1048576 | tf_op jit(solution)/shard_map/all_to_all | solution.py:101
  81.7 69.1 %all-reduce.7.cloned.1.call-start = ((), (), s32[]{:S(2)}) async-start(), calls=%async_computation.4 | async-start | bytes 1310720 | tf_op jit(solution)/shard_map/psum | solution.py:104
  102.4 22.5 %copy-start.9 = (s32[32,2]{0,1:T(2,128)S(1)}, s32[32,2]{0,1:T(2,128)}, u32[]{:S(2)}) copy-start(s32[32,2]{0,1:T(2,128)} %param.21) | copy-start | bytes 772
  102.4 22.7 %copy-start.4 = (bf16[2048,128]{1,0:T(8,128)(2,1)S(1)}, bf16[2048,128]{1,0:T(8,128)(2,1)}, u32[]{:S(2)}) copy-start(bf16[2048,128]{1,0:T(8,128)(2,1)} %param.34) | copy-start | bytes 1572868
  123.7 52.5 %copy-start.1 = (bf16[2048,256]{1,0:T(8,128)(2,1)S(1)}, bf16[2048,256]{1,0:T(8,128)(2,1)}, u32[]{:S(2)}) copy-start(bf16[2048,256]{1,0:T(8,128)(2,1)} %param.28) | copy-start | bytes 3145732
  150.8 24.6 %copy-start.8 = (bf16[32,2048]{1,0:T(8,128)(2,1)S(1)}, bf16[32,2048]{1,0:T(8,128)(2,1)}, u32[]{:S(2)}) copy-start(bf16[32,2048]{1,0:T(8,128)(2,1)} %get-tuple-element.22) | copy-start | bytes 393220
  150.8 22.6 %all-to-all-start.2 = ((bf16[64,2,2048]{2,1,0:T(2,128)(2,1)}), bf16[64,2,2048]{2,1,0:T(2,128)(2,1)S(1)}, u32[]{:S(2)}, u32[]{:S(2)}) async-start(bf16[64,2,2048]{2,1,0:T(2,128)(2,1)} %get-tuple-element.21), calls=%async_computation.2 | async-start | bytes 1048576 | tf_op jit(solution)/shard_map/all_to_all | solution.py:105
Sparse Core Ops, SparseCore 0:
  43.0 25.3 all-reduce.4
  125.0 25.7 all-reduce.6
where the time goes:
time: 184 us; the launch traced here: 183 us
  waiting for transfers between devices  51.2 us (28%)
  matrix products  35.5 us (19%)
  starting transfers between devices  32.6 us (18%)
  other arithmetic  19.4 us (11%)
  Pallas kernels  16.8 us (9%)
  between operations  14.5 us (8%)
  local copies, waits for them, and re-layouts  13 us (7%)
    psum x1, waiting for transfers between devices, local_layer(): expert_sum = lax.psum(expert_part, 'tp')  25.2 us
    another operation x3, Pallas kernels  15.6 us
    psum x1, waiting for transfers between devices, local_layer(): lax.psum(jnp.dot(attn_mix, w_o, preferred_element_type=jnp.float32).astyp...  14.8 us
    dot_general x1, matrix products, dense_block(): return jnp.dot(act_val, w_down, preferred_element_type=jnp.float32)  13.3 us
    all_to_all x1, starting transfers between devices, local_layer(): recv_expert = lax.all_to_all(send_expert, 'ep', 0, 0, tiled=True)  12 us
    all_to_all x1, waiting for transfers between devices, local_layer(): returned = lax.all_to_all(expert_sum, 'ep', 0, 0, tiled=True)  11.2 us
    all_to_all x1, starting transfers between devices, local_layer(): returned = lax.all_to_all(expert_sum, 'ep', 0, 0, tiled=True)  10.3 us
    all_to_all x1, starting transfers between devices, local_layer(): recv_rows = lax.all_to_all(send_rows, 'ep', 0, 0, tiled=True)  10.1 us
  transfers between devices with their start and end apart: 5, of which 3 were waited for; matrix products, arithmetic and copies ran while one was open for 28% of the time, Pallas kernels for 1%

commit v1 on v0

v1 whole, which is shorter than its diff:
```python
import functools
import math

import jax
import jax.numpy as jnp
from jax import lax
from jax.experimental import pallas as pl
from jax.experimental.pallas import tpu as pltpu
from jax.sharding import PartitionSpec as P

NORM_EPS = 1e-5
ROPE_BASE = 10000.0
MESH = pl.DeviceIdType.MESH
F32 = jnp.float32
BF16 = jnp.bfloat16


def iota(shape, axis):
    return lax.broadcasted_iota(jnp.int32, shape, axis)


def gain_row(ref):
    tile = ref[...].astype(F32)
    return jnp.concatenate([tile[i:i + 1, :] for i in range(tile.shape[0])], axis=1)


def inv_rms(wide):
    return lax.rsqrt(jnp.mean(wide * wide, axis=-1, keepdims=True) + NORM_EPS)


def silu_mul(gate, up):
    return ((gate * jax.nn.sigmoid(gate)) * up).astype(BF16)


def layer_kernel(dims, x_h, pos_h, ids_h, kc_h, vc_h, gin_h, gres_h, gpost_h, wq_h, wk_h, wv_h, wo_h, wg_h, wu_h, wd_h, wr_h,
                 eg_h, eu_h, ed_h, out_h, ko_h, vo_h,
                 x_v, pos_v, ids_v, kc_v, vc_v, gin_v, gres_v, gpost_v, wq_v, wk_v, wv_v, wo_v, wg_v, wu_v, wr_v,
                 eg_v, eu_v, ed_v, ko_v, vo_v, a_v, q_v, mix_v, as_v, ar_v, h_v, c_v, act_v, den_v,
                 ds_v, dr_v, rows_v, z_v, rs_v, rr_v, ret_v, fs_v, fr_v, out_v,
                 small_sem, w_sem, out_sem, tp_sem, ep_sem):
    T, D, L, KV, HD, QH, F, EL, EF, EP, CAP, TILE = dims
    group = QH // KV
    slots = EP * CAP
    me = lax.axis_index('ep')
    other = 1 - lax.axis_index('tp')

    barrier = pltpu.get_barrier_semaphore()

    def signal_peer(i, carry):
        pl.semaphore_signal(barrier, inc=1, device_id={'ep': lax.rem(me + i, EP)}, device_id_type=MESH)
        return carry

    lax.fori_loop(1, EP, signal_peer, 0)
    pl.semaphore_signal(barrier, inc=1, device_id={'tp': other}, device_id_type=MESH)

    small = [(x_h, x_v), (pos_h, pos_v), (ids_h, ids_v), (gin_h, gin_v), (gres_h, gres_v), (gpost_h, gpost_v)]
    for i, (src, dst) in enumerate(small):
        pltpu.make_async_copy(src, dst, small_sem.at[i]).start()

    def fetch(src, dst, sem, parts):
        step = dst.shape[0] // parts
        for i in range(parts):
            rows = pl.ds(i * step, step)
            pltpu.make_async_copy(src.at[rows], dst.at[rows], sem).start()

    def arrive(dst, sem):
        pltpu.make_async_copy(dst, dst, sem).wait()

    fetch(wr_h, wr_v, w_sem.at[0], 1)
    fetch(wk_h, wk_v, w_sem.at[1], 1)
    fetch(wv_h, wv_v, w_sem.at[2], 1)
    fetch(wq_h, wq_v, w_sem.at[3], 4)
    fetch(kc_h, kc_v, w_sem.at[4], 1)
    fetch(vc_h, vc_v, w_sem.at[5], 1)
    fetch(wo_h, wo_v, w_sem.at[6], 4)
    fetch(eg_h, eg_v, w_sem.at[7], EL)
    fetch(eu_h, eu_v, w_sem.at[8], EL)
    fetch(ed_h, ed_v, w_sem.at[9], EL)

    for i, (src, dst) in enumerate(small):
        pltpu.make_async_copy(src, dst, small_sem.at[i]).wait()

    wide = x_v[...].astype(F32)
    scaled = wide * inv_rms(wide)
    a_v[...] = (scaled * gain_row(gin_v)).astype(BF16)
    moe_in = (scaled * gain_row(gpost_v)).astype(BF16)

    eye = iota((T, T), 0) == iota((T, T), 1)
    before = iota((T, T), 0) < iota((T, T), 1)

    def to_col(row):
        return jnp.sum(jnp.where(eye, row, 0.0), axis=1, keepdims=True)

    ids = ids_v[...]
    pos_row = pos_v[...].astype(F32)
    pos_col = to_col(pos_row)
    id_rows = [ids[k:k + 1, :].astype(F32) for k in range(2)]
    dest_rows = [jnp.floor(r * (1.0 / EL)) for r in id_rows]
    bit_rows = [r - EL * d for r, d in zip(id_rows, dest_rows)]
    dest_cols = [to_col(d) for d in dest_rows]
    rank0 = jnp.sum(jnp.where((dest_cols[0] == dest_rows[0]) & before, 1.0, 0.0), axis=0, keepdims=True)
    rank1 = (jnp.sum(jnp.where(dest_cols[0] == dest_rows[1], 1.0, 0.0), axis=0, keepdims=True)
             + jnp.sum(jnp.where((dest_cols[1] == dest_rows[1]) & before, 1.0, 0.0), axis=0, keepdims=True))
    slot_rows = [dest_rows[0] * CAP + rank0, dest_rows[1] * CAP + rank1]
    slot_cols = [to_col(s) for s in slot_rows]
    slot_iota = iota((slots, T), 0).astype(F32)
    hot = [jnp.where(slot_iota == s, 1.0, 0.0) for s in slot_rows]
    which = jnp.sum(hot[0] * bit_rows[0] + hot[1] * bit_rows[1], axis=1, keepdims=True)
    sent = jnp.dot((hot[0] + hot[1]).astype(BF16), moe_in, preferred_element_type=F32).astype(BF16)
    ds_v[:, :, :D] = sent.reshape(EP, CAP, D)
    ds_v[:, :, D:] = jnp.broadcast_to(which, (slots, 128)).astype(BF16).reshape(EP, CAP, 128)
    dr_v[me] = ds_v[me]

    arrive(wr_v, w_sem.at[0])
    logits = jnp.dot(moe_in, wr_v[...], preferred_element_type=F32)
    expd = jnp.exp(logits - jnp.max(logits, axis=-1, keepdims=True))
    probs = expd / jnp.sum(expd, axis=-1, keepdims=True)
    lane = iota(logits.shape, 1).astype(F32)
    picked = [jnp.sum(jnp.where(lane == to_col(r), probs, 0.0), axis=1, keepdims=True) for r in id_rows]
    total = picked[0] + picked[1]
    weights = [pk / total for pk in picked]

    pl.semaphore_wait(barrier, EP)

    def send_rows(i, carry):
        peer = lax.rem(me + i, EP)
        pltpu.make_async_remote_copy(src_ref=ds_v.at[peer], dst_ref=dr_v.at[me], send_sem=ep_sem.at[0], recv_sem=ep_sem.at[1],
                                     device_id={'ep': peer}, device_id_type=MESH).start()
        return carry

    lax.fori_loop(1, EP, send_rows, 0)

    def tiled(width, body, tile=TILE):
        tile = min(tile, width)

        def step(i, carry):
            body(pl.ds(pl.multiple_of(i * tile, tile), tile))
            return carry

        lax.fori_loop(0, width // tile, step, 0)

    inv_freq = jnp.exp((iota((1, HD), 1) & (HD // 2 - 1)).astype(F32) * (-2.0 / HD * math.log(ROPE_BASE)))
    angles = pos_col * inv_freq
    cosine = jnp.cos(angles)
    sine = jnp.where(iota((1, HD), 1) < HD // 2, -1.0, 1.0) * jnp.sin(angles)

    def rope(head):
        return (head * cosine + pltpu.roll(head, HD // 2, 1) * sine).astype(BF16)

    arrive(wk_v, w_sem.at[1])
    k_proj = jnp.dot(a_v[...], wk_v[...], preferred_element_type=F32)
    k_new = jnp.concatenate([rope(k_proj[:, g * HD:(g + 1) * HD]) for g in range(KV)], axis=0)
    arrive(wv_v, w_sem.at[2])
    v_proj = jnp.dot(a_v[...], wv_v[...], preferred_element_type=F32).astype(BF16)
    v_new = jnp.concatenate([v_proj[:, g * HD:(g + 1) * HD] for g in range(KV)], axis=0)

    arrive(wq_v, w_sem.at[3])

    def q_tile(cols):
        q_v[:, cols] = jnp.dot(a_v[...], wq_v[:, cols], preferred_element_type=F32)

    tiled(QH * HD, q_tile)
    fetch(wg_h, wg_v, w_sem.at[10], 4)
    fetch(wu_h, wu_v, w_sem.at[11], 4)
    half = min(wd_h.shape[0], wq_v.shape[0])
    rest = wd_h.shape[0] - half
    pltpu.make_async_copy(wd_h.at[pl.ds(0, half)], wq_v.at[pl.ds(0, half)], w_sem.at[12]).start()

    arrive(kc_v, w_sem.at[4])
    arrive(vc_v, w_sem.at[5])
    tok_i = iota((T, KV * T), 0)
    lane_j = iota((T, KV * T), 1)
    target = jnp.sum(jnp.where(lax.rem(lane_j, T) == tok_i, (tok_i.astype(F32) * L + pos_col) * KV, 0.0), axis=0, keepdims=True)
    target = target + jnp.floor(iota((1, KV * T), 1).astype(F32) * (1.0 / T))
    new_rows = jnp.concatenate([k_new, v_new, jnp.ones((KV * T, HD), BF16)], axis=1)
    q_heads = [rope(q_v[:, h * HD:(h + 1) * HD]) for h in range(QH)]
    TC = min(16, T)
    width = TC * L * KV
    for c in range(T // TC):
        rows = pl.ds(c * width, width)
        place = jnp.where(iota((width, KV * T), 0).astype(F32) + float(c * width) == target, 1.0, 0.0).astype(BF16)
        placed = jnp.dot(place, new_rows, preferred_element_type=F32)
        hit = placed[:, 2 * HD:] > 0.5
        k_all = jnp.where(hit, placed[:, :HD], kc_v[rows, :].astype(F32)).astype(BF16)
        v_all = jnp.where(hit, placed[:, HD:2 * HD], vc_v[rows, :].astype(F32)).astype(BF16)
        ko_v[rows, :] = k_all
        vo_v[rows, :] = v_all
        q_rows = jnp.concatenate([q[c * TC:(c + 1) * TC] for q in q_heads], axis=0)
        scores = lax.dot_general(q_rows, k_all, (((1,), (1,)), ((), ())), preferred_element_type=F32) * (HD ** -0.5)
        head_kv = iota((QH * TC, 1), 0) // (group * TC)
        base = lax.rem(iota((QH * TC, 1), 0), TC) * (L * KV) + head_kv
        pos_rows = jnp.concatenate([pos_col[c * TC:(c + 1) * TC]] * QH, axis=0).astype(jnp.int32)
        last = base + KV * pos_rows
        col = iota((QH * TC, width), 1)
        visible = (col >= base) & (col <= last) & (lax.rem(col, KV) == head_kv)
        scores = jnp.where(visible, scores, -jnp.inf)
        expo = jnp.exp(scores - jnp.max(scores, axis=-1, keepdims=True))
        attn = (expo / jnp.sum(expo, axis=-1, keepdims=True)).astype(BF16)
        mixed = jnp.dot(attn, v_all, preferred_element_type=F32).astype(BF16)
        mix_v[c * TC:(c + 1) * TC, :] = jnp.concatenate([mixed[h * TC:(h + 1) * TC] for h in range(QH)], axis=1)
    cache_out = [pltpu.make_async_copy(ko_v, ko_h, out_sem.at[0]), pltpu.make_async_copy(vo_v, vo_h, out_sem.at[1])]
    for copy in cache_out:
        copy.start()

    arrive(wo_v, w_sem.at[6])

    def o_tile(cols):
        as_v[:, cols] = jnp.dot(mix_v[...], wo_v[:, cols], preferred_element_type=F32).astype(BF16)

    tiled(D, o_tile)
    if rest:
        pltpu.make_async_copy(wd_h.at[pl.ds(half, rest)], wo_v.at[pl.ds(0, rest)], w_sem.at[13]).start()
    attn_copy = pltpu.make_async_remote_copy(src_ref=as_v, dst_ref=ar_v, send_sem=tp_sem.at[0], recv_sem=tp_sem.at[1],
                                             device_id={'tp': other}, device_id_type=MESH)
    attn_copy.start()
    attn_copy.wait()
    mid = (x_v[...].astype(F32) + (as_v[...].astype(F32) + ar_v[...].astype(F32))).astype(BF16)
    h_v[...] = mid
    mid = mid.astype(F32)
    c_v[...] = (mid * inv_rms(mid) * gain_row(gres_v)).astype(BF16)

    arrive(wg_v, w_sem.at[10])
    arrive(wu_v, w_sem.at[11])

    def ff_tile(cols):
        gate = jnp.dot(c_v[...], wg_v[:, cols], preferred_element_type=F32)
        up = jnp.dot(c_v[...], wu_v[:, cols], preferred_element_type=F32)
        act_v[:, cols] = silu_mul(gate, up)

    tiled(F, ff_tile)

    arrive(eg_v, w_sem.at[7])
    arrive(eu_v, w_sem.at[8])
    arrive(ed_v, w_sem.at[9])
    others = pl.ds(0, EP - 1)
    pltpu.make_async_copy(dr_v.at[others], dr_v.at[others], ep_sem.at[1]).wait()
    rows_v[...] = dr_v[...].reshape(slots, D + 128)
    for e in range(EL):
        gate = jnp.dot(rows_v[:, :D], eg_v[e], preferred_element_type=F32)
        up = jnp.dot(rows_v[:, :D], eu_v[e], preferred_element_type=F32)
        mine = rows_v[:, D:D + 1].astype(F32) == float(e)
        z_v[:, e * EF:(e + 1) * EF] = jnp.where(mine, silu_mul(gate, up).astype(F32), 0.0).astype(BF16)

    def back_tile(cols):
        part = jnp.dot(z_v[:, :EF], ed_v[0, :, cols], preferred_element_type=F32)
        for e in range(1, EL):
            part += jnp.dot(z_v[:, e * EF:(e + 1) * EF], ed_v[e, :, cols], preferred_element_type=F32)
        rs_v[:, :, cols] = part.astype(BF16).reshape(EP, CAP, part.shape[1])

    tiled(D, back_tile)
    rr_v[me] = rs_v[me]

    def send_back(i, carry):
        peer = lax.rem(me + i, EP)
        pltpu.make_async_remote_copy(src_ref=rs_v.at[peer], dst_ref=rr_v.at[me], send_sem=ep_sem.at[2], recv_sem=ep_sem.at[3],
                                     device_id={'ep': peer}, device_id_type=MESH).start()
        return carry

    lax.fori_loop(1, EP, send_back, 0)

    arrive(wq_v.at[pl.ds(0, half)], w_sem.at[12])
    if rest:
        arrive(wo_v.at[pl.ds(0, rest)], w_sem.at[13])

    def down_tile(cols):
        part = jnp.dot(act_v[:, :half], wq_v[:half, cols], preferred_element_type=F32)
        if rest:
            part += jnp.dot(act_v[:, half:], wo_v[:rest, cols], preferred_element_type=F32)
        den_v[:, cols] = part

    tiled(D, down_tile)

    pltpu.make_async_copy(rr_v.at[others], rr_v.at[others], ep_sem.at[3]).wait()
    ret_v[...] = rr_v[...].reshape(slots, D)
    slot_lane = iota((T, slots), 1).astype(F32)
    take = [jnp.where(slot_lane == s, 1.0, 0.0).astype(BF16) for s in slot_cols]

    def sum_tile(cols):
        moe = weights[0] * jnp.dot(take[0], ret_v[:, cols], preferred_element_type=F32)
        moe += weights[1] * jnp.dot(take[1], ret_v[:, cols], preferred_element_type=F32)
        fs_v[:, cols] = (den_v[:, cols] + moe).astype(BF16)

    tiled(D, sum_tile)
    last_copy = pltpu.make_async_remote_copy(src_ref=fs_v, dst_ref=fr_v, send_sem=tp_sem.at[2], recv_sem=tp_sem.at[3],
                                             device_id={'tp': other}, device_id_type=MESH)
    last_copy.start()
    last_copy.wait()
    out_v[...] = (h_v[...].astype(F32) + (fs_v[...].astype(F32) + fr_v[...].astype(F32))).astype(BF16)
    done = pltpu.make_async_copy(out_v, out_h, out_sem.at[2])
    done.start()
    for sem, ref in ((0, ds_v), (2, rs_v)):
        pltpu.make_async_copy(ref.at[others], ref.at[others], ep_sem.at[sem]).wait()
    for copy in cache_out:
        copy.wait()
    done.wait()


def solution(mesh):
    EP = mesh.shape['ep']
    row_spec = P(('dp', 'ep'), None)
    cache_spec = P(('dp', 'ep'), None, 'tp', None)
    col_split = P(None, 'tp')
    row_split = P('tp', None)
    in_specs = (row_spec, P(('dp', 'ep')), row_spec, cache_spec, cache_spec, P(None), P(None), P(None), col_split, col_split, col_split, row_split, col_split, col_split, row_split, P(None, None), P('ep', None, 'tp'), P('ep', None, 'tp'), P('ep', 'tp', None))
    out_specs = (row_spec, cache_spec, cache_spec)

    def local_layer(hidden_in, positions, expert_ids, k_cache, v_cache, norm_in, norm_res, norm_post, w_q, w_k, w_v, w_o, w_gate, w_up, w_down, w_router, e_gate, e_up, e_down):
        T, D = hidden_in.shape
        _, L, KV, HD = k_cache.shape
        QH = w_q.shape[1] // HD
        F = w_gate.shape[1]
        EL, _, EF = e_gate.shape
        CAP = 4 * T // EP
        dims = (T, D, L, KV, HD, QH, F, EL, EF, EP, CAP, 512)
        slots = EP * CAP
        cache_rows = (T * L * KV, HD)
        args = (hidden_in, positions.reshape(1, T), expert_ids.T, k_cache.reshape(cache_rows), v_cache.reshape(cache_rows),
                norm_in.reshape(D // 128, 128), norm_res.reshape(D // 128, 128), norm_post.reshape(D // 128, 128),
                w_q, w_k, w_v, w_o, w_gate, w_up, w_down, w_router, e_gate, e_up, e_down)
        mirror = [pltpu.VMEM(a.shape, a.dtype) for i, a in enumerate(args) if i != 14]
        work = [
            pltpu.VMEM(cache_rows, BF16), pltpu.VMEM(cache_rows, BF16),
            pltpu.VMEM((T, D), BF16), pltpu.VMEM((T, QH * HD), F32), pltpu.VMEM((T, QH * HD), BF16),
            pltpu.VMEM((T, D), BF16), pltpu.VMEM((T, D), BF16), pltpu.VMEM((T, D), BF16), pltpu.VMEM((T, D), BF16),
            pltpu.VMEM((T, F), BF16), pltpu.VMEM((T, D), F32),
            pltpu.VMEM((EP, CAP, D + 128), BF16), pltpu.VMEM((EP, CAP, D + 128), BF16), pltpu.VMEM((slots, D + 128), BF16),
            pltpu.VMEM((slots, EL * EF), BF16), pltpu.VMEM((EP, CAP, D), BF16), pltpu.VMEM((EP, CAP, D), BF16), pltpu.VMEM((slots, D), BF16),
            pltpu.VMEM((T, D), BF16), pltpu.VMEM((T, D), BF16), pltpu.VMEM((T, D), BF16),
            pltpu.SemaphoreType.DMA((6,)), pltpu.SemaphoreType.DMA((14,)), pltpu.SemaphoreType.DMA((3,)),
            pltpu.SemaphoreType.DMA((4,)), pltpu.SemaphoreType.DMA((4,)),
        ]
        hbm = pl.BlockSpec(memory_space=pl.ANY)
        out, k_out, v_out = pl.pallas_call(
            functools.partial(layer_kernel, dims),
            out_shape=(jax.ShapeDtypeStruct((T, D), BF16), jax.ShapeDtypeStruct(cache_rows, BF16), jax.ShapeDtypeStruct(cache_rows, BF16)),
            in_specs=[hbm] * len(args),
            out_specs=(hbm, hbm, hbm),
            scratch_shapes=mirror + work,
            compiler_params=pltpu.CompilerParams(collective_id=0, has_side_effects=True, vmem_limit_bytes=67043328),
            name='layer',
        )(*args)
        return out, k_out.reshape(k_cache.shape), v_out.reshape(v_cache.shape)

    return jax.shard_map(local_layer, mesh=mesh, in_specs=in_specs, out_specs=out_specs, check_vma=False)
```

time: 184 us -> 54 us (0.29)
  waiting for transfers between devices: 51.2 us -> 0 us
  matrix products: 35.5 us -> 0 us
  starting transfers between devices: 32.6 us -> 0 us
  Pallas kernels: 16.8 us -> 47 us
  other arithmetic: 19.4 us -> 0 us
  between operations: 14.5 us -> 0.65 us
  local copies, waits for them, and re-layouts: 13 us -> 6.12 us
    pallas_call x0 -> x1, Pallas kernels: none -> 47 us  [local_layer(): pl.pallas_call(functools.partial(layer_kernel, dims), out_shape=(jax.Shap...]
    psum x2 -> x0, waiting for transfers between devices: 40 us -> none  [the longest x1 25.2 us: local_layer(): expert_sum = lax.psum(expert_part, 'tp')]
    dot_general x9 -> x0, matrix products: 35.5 us -> none  [the longest x1 13.3 us: dense_block(): return jnp.dot(act_val, w_down, preferred_element_type=jnp.float32)]
    all_to_all x3 -> x0, starting transfers between devices: 32.3 us -> none  [the longest x1 12 us: local_layer(): recv_expert = lax.all_to_all(send_expert, 'ep', 0, 0, tiled=True)]
    another operation x3 -> x0, Pallas kernels: 15.6 us -> none
    all_to_all x3 -> x0, waiting for transfers between devices: 11.2 us -> none  [the longest x1 11.2 us: local_layer(): returned = lax.all_to_all(expert_sum, 'ep', 0, 0, tiled=True)]
    gather x9 -> x0, local copies, waits for them, and re-layouts: 5.49 us -> none  [the longest x1 1.72 us: run_experts(): sorted_rows = slot_rows[sort_order]]
    convert_element_type x8 -> x0, other arithmetic: 5.14 us -> none  [the longest x1 1.73 us: run_experts(): act_val = (jax.nn.silu(gate_val) * up_val).astype(jnp.bfloat16)]
  transfers between devices with their start and end apart: 5 -> 0, of which waited for: 3 -> 0; matrix products, arithmetic and copies ran while one was open for 28% -> 0% of each run, Pallas kernels for 1% -> 0%
where the time goes in v1:
time: 54 us; the launch traced here: 53.7 us
  Pallas kernels  47 us (87%)
  local copies, waits for them, and re-layouts  6.12 us (11%)
  between operations  0.65 us (1%)
    pallas_call x1, Pallas kernels, local_layer(): pl.pallas_call(functools.partial(layer_kernel, dims), out_shape=(jax.Shap...  47 us
    unnamed x3, local copies, waits for them, and re-layouts  6.12 us

profile of v1, /device:TPU:1, one launch (start us, length us, event | category | flops | bytes accessed | tf_op | source)
XLA Modules:
  0.0 53.7 jit_solution(4846014142256939853)
XLA Ops:
  0.6 47.0 %layer.1 = (bf16[32,2048]{1,0:T(8,128)(2,1)}, bf16[2048,128]{1,0:T(8,128)(2,1)}, bf16[2048,128]{1,0:T(8,128)(2,1)}) custom-call(bf16[32,2048]{1,0:T(8,128)(2,1)} %x_h.1, s32[1,32]{1,0:T(1,128)} %bitcast.17, s32[2,32]{1,0:T(2,128)} %bitcast.16, bf16[2048,128]{1,0:T(8,128)(2,1)} %bitcast.9, bf16[2048,128]{1,0:T(8,128)(2,1)} %bitcast.10, ...), custom_call_target="tpu_custom_call" | custom-call | tf_op jit(solution)/shard_map/layer/pallas_call | solution.py:333
  47.6 1.6 %copy.25 = bf16[32,2048]{1,0:T(8,128)(2,1)} copy(bf16[32,2048]{1,0:T(8,128)(2,1)} %get-tuple-element.12) | data formatting | bytes 262144
  49.2 2.3 %copy.26 = bf16[32,32,2,128]{3,2,1,0:T(2,128)(2,1)} copy(bf16[32,32,2,128]{3,2,1,0:T(2,128)(2,1)} %bitcast.12) | data formatting | bytes 1048576
  51.5 2.3 %copy.27 = bf16[32,32,2,128]{3,2,1,0:T(2,128)(2,1)} copy(bf16[32,32,2,128]{3,2,1,0:T(2,128)(2,1)} %bitcast.11) | data formatting | bytes 1048576

commit v2 on v1

--- a/solution.py
+++ b/solution.py
@@ -35,14 +35,16 @@
 def layer_kernel(dims, x_h, pos_h, ids_h, kc_h, vc_h, gin_h, gres_h, gpost_h, wq_h, wk_h, wv_h, wo_h, wg_h, wu_h, wd_h, wr_h,
                  eg_h, eu_h, ed_h, out_h, ko_h, vo_h,
                  x_v, pos_v, ids_v, kc_v, vc_v, gin_v, gres_v, gpost_v, wq_v, wk_v, wv_v, wo_v, wg_v, wu_v, wr_v,
-                 eg_v, eu_v, ed_v, ko_v, vo_v, a_v, q_v, mix_v, as_v, ar_v, h_v, c_v, act_v, den_v,
-                 ds_v, dr_v, rows_v, z_v, rs_v, rr_v, ret_v, fs_v, fr_v, out_v,
+                 eg_v, eu_v, ed_v, ko_v, vo_v, a_v, m_v, q_v, mix_v, as_v, ar_v, h_v, c_v, act_v, den_v,
+                 ds_v, dr_v, dp_v, near_v, far_v, gu_v, z_v, xs_v, xr_v, own_v, rs_v, rr_v, ret_v, fs_v, fr_v, out_v,
                  small_sem, w_sem, out_sem, tp_sem, ep_sem):
     T, D, L, KV, HD, QH, F, EL, EF, EP, CAP, TILE = dims
     group = QH // KV
     slots = EP * CAP
     me = lax.axis_index('ep')
-    other = 1 - lax.axis_index('tp')
+    mine = lax.axis_index('tp')
+    other = 1 - mine
+    HALF = D // 2
 
     barrier = pltpu.get_barrier_semaphore()
 
@@ -84,6 +86,9 @@
     scaled = wide * inv_rms(wide)
     a_v[...] = (scaled * gain_row(gin_v)).astype(BF16)
     moe_in = (scaled * gain_row(gpost_v)).astype(BF16)
+    m_v[...] = moe_in
+    mine_half = pl.ds(pl.multiple_of(mine * HALF, HALF), HALF)
+    other_half = pl.ds(pl.multiple_of(other * HALF, HALF), HALF)
 
     eye = iota((T, T), 0) == iota((T, T), 1)
     before = iota((T, T), 0) < iota((T, T), 1)
@@ -106,9 +111,9 @@
     slot_iota = iota((slots, T), 0).astype(F32)
     hot = [jnp.where(slot_iota == s, 1.0, 0.0) for s in slot_rows]
     which = jnp.sum(hot[0] * bit_rows[0] + hot[1] * bit_rows[1], axis=1, keepdims=True)
-    sent = jnp.dot((hot[0] + hot[1]).astype(BF16), moe_in, preferred_element_type=F32).astype(BF16)
-    ds_v[:, :, :D] = sent.reshape(EP, CAP, D)
-    ds_v[:, :, D:] = jnp.broadcast_to(which, (slots, 128)).astype(BF16).reshape(EP, CAP, 128)
+    sent = jnp.dot((hot[0] + hot[1]).astype(BF16), m_v[:, mine_half], preferred_element_type=F32).astype(BF16)
+    ds_v[:, :, :HALF] = sent.reshape(EP, CAP, HALF)
+    ds_v[:, :, HALF:] = jnp.broadcast_to(which, (slots, 128)).astype(BF16).reshape(EP, CAP, 128)
     dr_v[me] = ds_v[me]
 
     arrive(wr_v, w_sem.at[0])
@@ -219,35 +224,39 @@
     mid = mid.astype(F32)
     c_v[...] = (mid * inv_rms(mid) * gain_row(gres_v)).astype(BF16)
 
-    arrive(wg_v, w_sem.at[10])
-    arrive(wu_v, w_sem.at[11])
-
-    def ff_tile(cols):
-        gate = jnp.dot(c_v[...], wg_v[:, cols], preferred_element_type=F32)
-        up = jnp.dot(c_v[...], wu_v[:, cols], preferred_element_type=F32)
-        act_v[:, cols] = silu_mul(gate, up)
-
-    tiled(F, ff_tile)
-
     arrive(eg_v, w_sem.at[7])
     arrive(eu_v, w_sem.at[8])
-    arrive(ed_v, w_sem.at[9])
     others = pl.ds(0, EP - 1)
     pltpu.make_async_copy(dr_v.at[others], dr_v.at[others], ep_sem.at[1]).wait()
-    rows_v[...] = dr_v[...].reshape(slots, D + 128)
+    rows_copy = pltpu.make_async_remote_copy(src_ref=dr_v, dst_ref=dp_v, send_sem=tp_sem.at[4], recv_sem=tp_sem.at[5],
+                                             device_id={'tp': other}, device_id_type=MESH)
+    rows_copy.start()
+    near_v[...] = dr_v[...].reshape(slots, HALF + 128)
     for e in range(EL):
-        gate = jnp.dot(rows_v[:, :D], eg_v[e], preferred_element_type=F32)
-        up = jnp.dot(rows_v[:, :D], eu_v[e], preferred_element_type=F32)
-        mine = rows_v[:, D:D + 1].astype(F32) == float(e)
-        z_v[:, e * EF:(e + 1) * EF] = jnp.where(mine, silu_mul(gate, up).astype(F32), 0.0).astype(BF16)
-
-    def back_tile(cols):
-        part = jnp.dot(z_v[:, :EF], ed_v[0, :, cols], preferred_element_type=F32)
+        gu_v[2 * e] = jnp.dot(near_v[:, :HALF], eg_v[e, mine_half, :], preferred_element_type=F32)
+        gu_v[2 * e + 1] = jnp.dot(near_v[:, :HALF], eu_v[e, mine_half, :], preferred_element_type=F32)
+    rows_copy.wait()
+    far_v[...] = dp_v[:, :, :HALF].reshape(slots, HALF)
+    for e in range(EL):
+        gate = gu_v[2 * e] + jnp.dot(far_v[...], eg_v[e, other_half, :], preferred_element_type=F32)
+        up = gu_v[2 * e + 1] + jnp.dot(far_v[...], eu_v[e, other_half, :], preferred_element_type=F32)
+        chosen = near_v[:, HALF:HALF + 1].astype(F32) == float(e)
+        z_v[:, e * EF:(e + 1) * EF] = jnp.where(chosen, silu_mul(gate, up).astype(F32), 0.0).astype(BF16)
+    arrive(ed_v, w_sem.at[9])
+
+    def expert_down(half):
+        part = jnp.dot(z_v[:, :EF], ed_v[0, :, half], preferred_element_type=F32)
         for e in range(1, EL):
-            part += jnp.dot(z_v[:, e * EF:(e + 1) * EF], ed_v[e, :, cols], preferred_element_type=F32)
-        rs_v[:, :, cols] = part.astype(BF16).reshape(EP, CAP, part.shape[1])
-
-    tiled(D, back_tile)
+            part += jnp.dot(z_v[:, e * EF:(e + 1) * EF], ed_v[e, :, half], preferred_element_type=F32)
+        return part
+
+    xs_v[...] = expert_down(other_half).astype(BF16)
+    sum_copy = pltpu.make_async_remote_copy(src_ref=xs_v, dst_ref=xr_v, send_sem=tp_sem.at[6], recv_sem=tp_sem.at[7],
+                                            device_id={'tp': other}, device_id_type=MESH)
+    sum_copy.start()
+    own_v[...] = expert_down(mine_half)
+    sum_copy.wait()
+    rs_v[...] = (own_v[...] + xr_v[...].astype(F32)).astype(BF16).reshape(EP, CAP, HALF)
     rr_v[me] = rs_v[me]
 
     def send_back(i, carry):
@@ -258,6 +267,16 @@
 
     lax.fori_loop(1, EP, send_back, 0)
 
+    arrive(wg_v, w_sem.at[10])
+    arrive(wu_v, w_sem.at[11])
+
+    def ff_tile(cols):
+        gate = jnp.dot(c_v[...], wg_v[:, cols], preferred_element_type=F32)
+        up = jnp.dot(c_v[...], wu_v[:, cols], preferred_element_type=F32)
+        act_v[:, cols] = silu_mul(gate, up)
+
+    tiled(F, ff_tile)
+
     arrive(wq_v.at[pl.ds(0, half)], w_sem.at[12])
     if rest:
         arrive(wo_v.at[pl.ds(0, rest)], w_sem.at[13])
@@ -267,20 +286,17 @@
         if rest:
             part += jnp.dot(act_v[:, half:], wo_v[:rest, cols], preferred_element_type=F32)
         den_v[:, cols] = part
+        fs_v[:, cols] = part.astype(BF16)
 
     tiled(D, down_tile)
 
     pltpu.make_async_copy(rr_v.at[others], rr_v.at[others], ep_sem.at[3]).wait()
-    ret_v[...] = rr_v[...].reshape(slots, D)
+    ret_v[...] = rr_v[...].reshape(slots, HALF)
     slot_lane = iota((T, slots), 1).astype(F32)
     take = [jnp.where(slot_lane == s, 1.0, 0.0).astype(BF16) for s in slot_cols]
-
-    def sum_tile(cols):
-        moe = weights[0] * jnp.dot(take[0], ret_v[:, cols], preferred_element_type=F32)
-        moe += weights[1] * jnp.dot(take[1], ret_v[:, cols], preferred_element_type=F32)
-        fs_v[:, cols] = (den_v[:, cols] + moe).astype(BF16)
-
-    tiled(D, sum_tile)
+    moe = weights[0] * jnp.dot(take[0], ret_v[...], preferred_element_type=F32)
+    moe += weights[1] * jnp.dot(take[1], ret_v[...], preferred_element_type=F32)
+    fs_v[:, mine_half] = (den_v[:, mine_half] + moe).astype(BF16)
     last_copy = pltpu.make_async_remote_copy(src_ref=fs_v, dst_ref=fr_v, send_sem=tp_sem.at[2], recv_sem=tp_sem.at[3],
                                              device_id={'tp': other}, device_id_type=MESH)
     last_copy.start()
@@ -295,6 +311,33 @@
     done.wait()
 
 
+def settle_kernel(*refs):
+    n = (len(refs) - 1) // 3
+    src, dst, buf, sem = refs[:n], refs[n:2 * n], refs[2 * n:3 * n], refs[-1]
+    loads = [pltpu.make_async_copy(s, b, sem.at[i]) for i, (s, b) in enumerate(zip(src, buf))]
+    stores = [pltpu.make_async_copy(b, d, sem.at[n + i]) for i, (b, d) in enumerate(zip(buf, dst))]
+    for copy in loads:
+        copy.start()
+    for load, store in zip(loads, stores):
+        load.wait()
+        store.start()
+    for copy in stores:
+        copy.wait()
+
+
+def settle(arrays):
+    hbm = pl.BlockSpec(memory_space=pl.ANY)
+    return pl.pallas_call(
+        settle_kernel,
+        out_shape=tuple(jax.ShapeDtypeStruct(a.shape, a.dtype) for a in arrays),
+        in_specs=[hbm] * len(arrays),
+        out_specs=(hbm,) * len(arrays),
+        scratch_shapes=[pltpu.VMEM(a.shape, a.dtype) for a in arrays] + [pltpu.SemaphoreType.DMA((2 * len(arrays),))],
+        compiler_params=pltpu.CompilerParams(vmem_limit_bytes=67043328),
+        name='settle',
+    )(*arrays)
+
+
 def solution(mesh):
     EP = mesh.shape['ep']
     row_spec = P(('dp', 'ep'), None)
@@ -313,6 +356,7 @@
         CAP = 4 * T // EP
         dims = (T, D, L, KV, HD, QH, F, EL, EF, EP, CAP, 512)
         slots = EP * CAP
+        HALF = D // 2
         cache_rows = (T * L * KV, HD)
         args = (hidden_in, positions.reshape(1, T), expert_ids.T, k_cache.reshape(cache_rows), v_cache.reshape(cache_rows),
                 norm_in.reshape(D // 128, 128), norm_res.reshape(D // 128, 128), norm_post.reshape(D // 128, 128),
@@ -320,14 +364,16 @@
         mirror = [pltpu.VMEM(a.shape, a.dtype) for i, a in enumerate(args) if i != 14]
         work = [
             pltpu.VMEM(cache_rows, BF16), pltpu.VMEM(cache_rows, BF16),
-            pltpu.VMEM((T, D), BF16), pltpu.VMEM((T, QH * HD), F32), pltpu.VMEM((T, QH * HD), BF16),
+            pltpu.VMEM((T, D), BF16), pltpu.VMEM((T, D), BF16), pltpu.VMEM((T, QH * HD), F32), pltpu.VMEM((T, QH * HD), BF16),
             pltpu.VMEM((T, D), BF16), pltpu.VMEM((T, D), BF16), pltpu.VMEM((T, D), BF16), pltpu.VMEM((T, D), BF16),
             pltpu.VMEM((T, F), BF16), pltpu.VMEM((T, D), F32),
-            pltpu.VMEM((EP, CAP, D + 128), BF16), pltpu.VMEM((EP, CAP, D + 128), BF16), pltpu.VMEM((slots, D + 128), BF16),
-            pltpu.VMEM((slots, EL * EF), BF16), pltpu.VMEM((EP, CAP, D), BF16), pltpu.VMEM((EP, CAP, D), BF16), pltpu.VMEM((slots, D), BF16),
+            pltpu.VMEM((EP, CAP, HALF + 128), BF16), pltpu.VMEM((EP, CAP, HALF + 128), BF16), pltpu.VMEM((EP, CAP, HALF + 128), BF16),
+            pltpu.VMEM((slots, HALF + 128), BF16), pltpu.VMEM((slots, HALF), BF16), pltpu.VMEM((2 * EL, slots, EF), F32),
+            pltpu.VMEM((slots, EL * EF), BF16), pltpu.VMEM((slots, HALF), BF16), pltpu.VMEM((slots, HALF), BF16), pltpu.VMEM((slots, HALF), F32),
+            pltpu.VMEM((EP, CAP, HALF), BF16), pltpu.VMEM((EP, CAP, HALF), BF16), pltpu.VMEM((slots, HALF), BF16),
             pltpu.VMEM((T, D), BF16), pltpu.VMEM((T, D), BF16), pltpu.VMEM((T, D), BF16),
             pltpu.SemaphoreType.DMA((6,)), pltpu.SemaphoreType.DMA((14,)), pltpu.SemaphoreType.DMA((3,)),
-            pltpu.SemaphoreType.DMA((4,)), pltpu.SemaphoreType.DMA((4,)),
+            pltpu.SemaphoreType.DMA((8,)), pltpu.SemaphoreType.DMA((4,)),
         ]
         hbm = pl.BlockSpec(memory_space=pl.ANY)
         out, k_out, v_out = pl.pallas_call(
@@ -339,6 +385,7 @@
             compiler_params=pltpu.CompilerParams(collective_id=0, has_side_effects=True, vmem_limit_bytes=67043328),
             name='layer',
         )(*args)
+        out, k_out, v_out = settle((out, k_out, v_out))
         return out, k_out.reshape(k_cache.shape), v_out.reshape(v_cache.shape)
 
     return jax.shard_map(local_layer, mesh=mesh, in_specs=in_specs, out_specs=out_specs, check_vma=False)

time: 54 us -> 41.8 us (0.77)
  local copies, waits for them, and re-layouts: 6.12 us -> 0 us
  Pallas kernels: 47 us -> 41 us
    pallas_call x1, Pallas kernels: 47 us -> 38.9 us  [local_layer(): pl.pallas_call(functools.partial(layer_kernel, dims), out_shape=(jax.Shap...]
    unnamed x3 -> x0, local copies, waits for them, and re-layouts: 6.12 us -> none
    pallas_call x0 -> x1, Pallas kernels: none -> 2.13 us  [settle(): pl.pallas_call(settle_kernel, out_shape=tuple((jax.ShapeDtypeStruct(a.sha...]
where the time goes in v2:
time: 41.8 us; the launch traced here: 41.7 us
  Pallas kernels  41 us (98%)
  between operations  0.65 us (2%)
    pallas_call x1, Pallas kernels, local_layer(): pl.pallas_call(functools.partial(layer_kernel, dims), out_shape=(jax.Shap...  38.9 us
    pallas_call x1, Pallas kernels, settle(): pl.pallas_call(settle_kernel, out_shape=tuple((jax.ShapeDtypeStruct(a.sha...  2.13 us

profile of v2, /device:TPU:1, one launch (start us, length us, event | category | flops | bytes accessed | tf_op | source)
XLA Modules:
  0.0 41.7 jit_solution(10920609955778938336)
XLA Ops:
  0.6 38.9 %layer.1 = (bf16[32,2048]{1,0:T(8,128)(2,1)}, bf16[2048,128]{1,0:T(8,128)(2,1)}, bf16[2048,128]{1,0:T(8,128)(2,1)}) custom-call(bf16[32,2048]{1,0:T(8,128)(2,1)} %x_h.1, s32[1,32]{1,0:T(1,128)} %bitcast.15, s32[2,32]{1,0:T(2,128)} %bitcast.14, bf16[2048,128]{1,0:T(8,128)(2,1)} %bitcast.9, bf16[2048,128]{1,0:T(8,128)(2,1)} %bitcast.10, ...), custom_call_target="tpu_custom_call" | custom-call | tf_op jit(solution)/shard_map/layer/pallas_call | solution.py:379
  39.6 2.1 %settle.1 = (bf16[32,2048]{1,0:T(8,128)(2,1)}, bf16[2048,128]{1,0:T(8,128)(2,1)}, bf16[2048,128]{1,0:T(8,128)(2,1)}) custom-call(bf16[32,2048]{1,0:T(8,128)(2,1)} %get-tuple-element.9.refs_0_, bf16[2048,128]{1,0:T(8,128)(2,1)} %get-tuple-element.10.refs_1_, bf16[2048,128]{1,0:T(8,128)(2,1)} %get-tuple-element.11.refs_2_), custom_call_target="tpu_custom_call" | custom-call | tf_op jit(solution)/shard_map/settle/pallas_call | solution.py:330

commit v3 on v2

--- a/solution.py
+++ b/solution.py
@@ -1,5 +1,6 @@
 import functools
 import math
+import random
 
 import jax
 import jax.numpy as jnp
@@ -17,6 +18,15 @@
 
 def iota(shape, axis):
     return lax.broadcasted_iota(jnp.int32, shape, axis)
+
+
+def peer_steps(n):
+    side = round(n ** (1 / 3))
+    if side ** 3 != n:
+        return n, [(0, 0, i) for i in range(1, n)]
+    steps = [(a, b, c) for a in range(side) for b in range(side) for c in range(side)][1:]
+    random.Random(1).shuffle(steps)
+    return side, sorted(steps, key=lambda s: -sum(min(d, side - d) for d in s))
 
 
 def gain_row(ref):
@@ -48,11 +58,13 @@
 
     barrier = pltpu.get_barrier_semaphore()
 
-    def signal_peer(i, carry):
-        pl.semaphore_signal(barrier, inc=1, device_id={'ep': lax.rem(me + i, EP)}, device_id_type=MESH)
-        return carry
-
-    lax.fori_loop(1, EP, signal_peer, 0)
+    side, steps = peer_steps(EP)
+    at = (lax.div(me, side * side), lax.rem(lax.div(me, side), side), lax.rem(me, side))
+    digit = [[lax.rem(p + d, side) * side ** (2 - axis) for d in range(side)] for axis, p in enumerate(at)]
+    peers = [digit[0][i] + digit[1][j] + digit[2][k] for i, j, k in steps]
+
+    for peer in peers:
+        pl.semaphore_signal(barrier, inc=1, device_id={'ep': peer}, device_id_type=MESH)
     pl.semaphore_signal(barrier, inc=1, device_id={'tp': other}, device_id_type=MESH)
 
     small = [(x_h, x_v), (pos_h, pos_v), (ids_h, ids_v), (gin_h, gin_v), (gres_h, gres_v), (gpost_h, gpost_v)]
@@ -114,7 +126,6 @@
     sent = jnp.dot((hot[0] + hot[1]).astype(BF16), m_v[:, mine_half], preferred_element_type=F32).astype(BF16)
     ds_v[:, :, :HALF] = sent.reshape(EP, CAP, HALF)
     ds_v[:, :, HALF:] = jnp.broadcast_to(which, (slots, 128)).astype(BF16).reshape(EP, CAP, 128)
-    dr_v[me] = ds_v[me]
 
     arrive(wr_v, w_sem.at[0])
     logits = jnp.dot(moe_in, wr_v[...], preferred_element_type=F32)
@@ -127,13 +138,13 @@
 
     pl.semaphore_wait(barrier, EP)
 
-    def send_rows(i, carry):
-        peer = lax.rem(me + i, EP)
-        pltpu.make_async_remote_copy(src_ref=ds_v.at[peer], dst_ref=dr_v.at[me], send_sem=ep_sem.at[0], recv_sem=ep_sem.at[1],
-                                     device_id={'ep': peer}, device_id_type=MESH).start()
-        return carry
-
-    lax.fori_loop(1, EP, send_rows, 0)
+    def exchange(src, dst, sem):
+        for peer in peers:
+            pltpu.make_async_remote_copy(src_ref=src.at[peer], dst_ref=dst.at[me], send_sem=ep_sem.at[sem], recv_sem=ep_sem.at[sem + 1],
+                                         device_id={'ep': peer}, device_id_type=MESH).start()
+
+    exchange(ds_v, dr_v, 0)
+    dr_v[me] = ds_v[me]
 
     def tiled(width, body, tile=TILE):
         tile = min(tile, width)
@@ -257,15 +268,8 @@
     own_v[...] = expert_down(mine_half)
     sum_copy.wait()
     rs_v[...] = (own_v[...] + xr_v[...].astype(F32)).astype(BF16).reshape(EP, CAP, HALF)
+    exchange(rs_v, rr_v, 2)
     rr_v[me] = rs_v[me]
-
-    def send_back(i, carry):
-        peer = lax.rem(me + i, EP)
-        pltpu.make_async_remote_copy(src_ref=rs_v.at[peer], dst_ref=rr_v.at[me], send_sem=ep_sem.at[2], recv_sem=ep_sem.at[3],
-                                     device_id={'ep': peer}, device_id_type=MESH).start()
-        return carry
-
-    lax.fori_loop(1, EP, send_back, 0)
 
     arrive(wg_v, w_sem.at[10])
     arrive(wu_v, w_sem.at[11])
@@ -285,57 +289,68 @@
         part = jnp.dot(act_v[:, :half], wq_v[:half, cols], preferred_element_type=F32)
         if rest:
             part += jnp.dot(act_v[:, half:], wo_v[:rest, cols], preferred_element_type=F32)
-        den_v[:, cols] = part
         fs_v[:, cols] = part.astype(BF16)
 
     tiled(D, down_tile)
+
+    dense_copy = pltpu.make_async_remote_copy(src_ref=fs_v, dst_ref=fr_v, send_sem=tp_sem.at[2], recv_sem=tp_sem.at[3],
+                                              device_id={'tp': other}, device_id_type=MESH)
+    dense_copy.start()
+    dense_copy.wait()
+    den_v[...] = h_v[:, mine_half].astype(F32) + (fs_v[:, mine_half].astype(F32) + fr_v[:, mine_half].astype(F32))
+    slot_lane = iota((T, slots), 1).astype(F32)
+    take = [jnp.where(slot_lane == s, 1.0, 0.0).astype(BF16) for s in slot_cols]
 
     pltpu.make_async_copy(rr_v.at[others], rr_v.at[others], ep_sem.at[3]).wait()
     ret_v[...] = rr_v[...].reshape(slots, HALF)
-    slot_lane = iota((T, slots), 1).astype(F32)
-    take = [jnp.where(slot_lane == s, 1.0, 0.0).astype(BF16) for s in slot_cols]
     moe = weights[0] * jnp.dot(take[0], ret_v[...], preferred_element_type=F32)
     moe += weights[1] * jnp.dot(take[1], ret_v[...], preferred_element_type=F32)
-    fs_v[:, mine_half] = (den_v[:, mine_half] + moe).astype(BF16)
-    last_copy = pltpu.make_async_remote_copy(src_ref=fs_v, dst_ref=fr_v, send_sem=tp_sem.at[2], recv_sem=tp_sem.at[3],
+    out_v[...] = (den_v[...] + moe).astype(BF16)
+    last_copy = pltpu.make_async_remote_copy(src_ref=out_v, dst_ref=out_h.at[mine], send_sem=tp_sem.at[8], recv_sem=tp_sem.at[9],
                                              device_id={'tp': other}, device_id_type=MESH)
     last_copy.start()
-    last_copy.wait()
-    out_v[...] = (h_v[...].astype(F32) + (fs_v[...].astype(F32) + fr_v[...].astype(F32))).astype(BF16)
-    done = pltpu.make_async_copy(out_v, out_h, out_sem.at[2])
+    done = pltpu.make_async_copy(out_v, out_h.at[mine], out_sem.at[2])
     done.start()
     for sem, ref in ((0, ds_v), (2, rs_v)):
         pltpu.make_async_copy(ref.at[others], ref.at[others], ep_sem.at[sem]).wait()
     for copy in cache_out:
         copy.wait()
+    last_copy.wait()
     done.wait()
 
 
-def settle_kernel(*refs):
-    n = (len(refs) - 1) // 3
-    src, dst, buf, sem = refs[:n], refs[n:2 * n], refs[2 * n:3 * n], refs[-1]
-    loads = [pltpu.make_async_copy(s, b, sem.at[i]) for i, (s, b) in enumerate(zip(src, buf))]
-    stores = [pltpu.make_async_copy(b, d, sem.at[n + i]) for i, (b, d) in enumerate(zip(buf, dst))]
-    for copy in loads:
+def settle_kernel(half_h, ki_h, vi_h, out_h, ko_h, vo_h, out_v, k_v, v_v, sem):
+    T, D = out_v.shape
+    cols = [pl.ds(0, D // 2), pl.ds(D // 2, D // 2)]
+    halves = [pltpu.make_async_copy(half_h.at[i], out_v.at[:, c], sem.at[i]) for i, c in enumerate(cols)]
+    loads = [pltpu.make_async_copy(ki_h, k_v, sem.at[2]), pltpu.make_async_copy(vi_h, v_v, sem.at[3])]
+    stores = [pltpu.make_async_copy(k_v, ko_h, sem.at[4]), pltpu.make_async_copy(v_v, vo_h, sem.at[5])]
+    last = pltpu.make_async_copy(out_v, out_h, sem.at[6])
+    for copy in loads + halves:
         copy.start()
     for load, store in zip(loads, stores):
         load.wait()
         store.start()
-    for copy in stores:
+    for copy in halves:
         copy.wait()
-
-
-def settle(arrays):
+    last.start()
+    for copy in stores + [last]:
+        copy.wait()
+
+
+def settle(halves, k_rows, v_rows):
     hbm = pl.BlockSpec(memory_space=pl.ANY)
+    T, D = halves.shape[1], 2 * halves.shape[2]
+    shapes = ((T, D), k_rows.shape, v_rows.shape)
     return pl.pallas_call(
         settle_kernel,
-        out_shape=tuple(jax.ShapeDtypeStruct(a.shape, a.dtype) for a in arrays),
-        in_specs=[hbm] * len(arrays),
-        out_specs=(hbm,) * len(arrays),
-        scratch_shapes=[pltpu.VMEM(a.shape, a.dtype) for a in arrays] + [pltpu.SemaphoreType.DMA((2 * len(arrays),))],
+        out_shape=tuple(jax.ShapeDtypeStruct(s, BF16) for s in shapes),
+        in_specs=[hbm] * 3,
+        out_specs=(hbm,) * 3,
+        scratch_shapes=[pltpu.VMEM(s, BF16) for s in shapes] + [pltpu.SemaphoreType.DMA((7,))],
         compiler_params=pltpu.CompilerParams(vmem_limit_bytes=67043328),
         name='settle',
-    )(*arrays)
+    )(halves, k_rows, v_rows)
 
 
 def solution(mesh):
@@ -366,26 +381,26 @@
             pltpu.VMEM(cache_rows, BF16), pltpu.VMEM(cache_rows, BF16),
             pltpu.VMEM((T, D), BF16), pltpu.VMEM((T, D), BF16), pltpu.VMEM((T, QH * HD), F32), pltpu.VMEM((T, QH * HD), BF16),
             pltpu.VMEM((T, D), BF16), pltpu.VMEM((T, D), BF16), pltpu.VMEM((T, D), BF16), pltpu.VMEM((T, D), BF16),
-            pltpu.VMEM((T, F), BF16), pltpu.VMEM((T, D), F32),
+            pltpu.VMEM((T, F), BF16), pltpu.VMEM((T, HALF), F32),
             pltpu.VMEM((EP, CAP, HALF + 128), BF16), pltpu.VMEM((EP, CAP, HALF + 128), BF16), pltpu.VMEM((EP, CAP, HALF + 128), BF16),
             pltpu.VMEM((slots, HALF + 128), BF16), pltpu.VMEM((slots, HALF), BF16), pltpu.VMEM((2 * EL, slots, EF), F32),
             pltpu.VMEM((slots, EL * EF), BF16), pltpu.VMEM((slots, HALF), BF16), pltpu.VMEM((slots, HALF), BF16), pltpu.VMEM((slots, HALF), F32),
             pltpu.VMEM((EP, CAP, HALF), BF16), pltpu.VMEM((EP, CAP, HALF), BF16), pltpu.VMEM((slots, HALF), BF16),
-            pltpu.VMEM((T, D), BF16), pltpu.VMEM((T, D), BF16), pltpu.VMEM((T, D), BF16),
+            pltpu.VMEM((T, D), BF16), pltpu.VMEM((T, D), BF16), pltpu.VMEM((T, HALF), BF16),
             pltpu.SemaphoreType.DMA((6,)), pltpu.SemaphoreType.DMA((14,)), pltpu.SemaphoreType.DMA((3,)),
-            pltpu.SemaphoreType.DMA((8,)), pltpu.SemaphoreType.DMA((4,)),
+            pltpu.SemaphoreType.DMA((10,)), pltpu.SemaphoreType.DMA((4,)),
         ]
         hbm = pl.BlockSpec(memory_space=pl.ANY)
         out, k_out, v_out = pl.pallas_call(
             functools.partial(layer_kernel, dims),
-            out_shape=(jax.ShapeDtypeStruct((T, D), BF16), jax.ShapeDtypeStruct(cache_rows, BF16), jax.ShapeDtypeStruct(cache_rows, BF16)),
+            out_shape=(jax.ShapeDtypeStruct((2, T, HALF), BF16), jax.ShapeDtypeStruct(cache_rows, BF16), jax.ShapeDtypeStruct(cache_rows, BF16)),
             in_specs=[hbm] * len(args),
             out_specs=(hbm, hbm, hbm),
             scratch_shapes=mirror + work,
             compiler_params=pltpu.CompilerParams(collective_id=0, has_side_effects=True, vmem_limit_bytes=67043328),
             name='layer',
         )(*args)
-        out, k_out, v_out = settle((out, k_out, v_out))
+        out, k_out, v_out = settle(out, k_out, v_out)
         return out, k_out.reshape(k_cache.shape), v_out.reshape(v_cache.shape)
 
     return jax.shard_map(local_layer, mesh=mesh, in_specs=in_specs, out_specs=out_specs, check_vma=False)

time: 41.8 us -> 40.9 us (0.978)
  Pallas kernels: 41 us -> 40.2 us
    pallas_call x1, Pallas kernels: 38.9 us -> 38.1 us  [local_layer(): pl.pallas_call(functools.partial(layer_kernel, dims), out_shape=(jax.Shap...]
where the time goes in v3:
time: 40.9 us; the launch traced here: 40.8 us
  Pallas kernels  40.2 us (98%)
  between operations  0.65 us (2%)
    pallas_call x1, Pallas kernels, local_layer(): pl.pallas_call(functools.partial(layer_kernel, dims), out_shape=(jax.Shap...  38.1 us
    pallas_call x1, Pallas kernels, settle(): pl.pallas_call(settle_kernel, out_shape=tuple((jax.ShapeDtypeStruct(s, BF...  2.1 us

profile of v3, /device:TPU:1, one launch (start us, length us, event | category | flops | bytes accessed | tf_op | source)
XLA Modules:
  0.0 40.8 jit_solution(3790245581481899303)
XLA Ops:
  0.6 38.1 %layer.1 = (bf16[2,32,1024]{2,1,0:T(8,128)(2,1)}, bf16[2048,128]{1,0:T(8,128)(2,1)}, bf16[2048,128]{1,0:T(8,128)(2,1)}) custom-call(bf16[32,2048]{1,0:T(8,128)(2,1)} %x_h.1, s32[1,32]{1,0:T(1,128)} %bitcast.15, s32[2,32]{1,0:T(2,128)} %bitcast.14, bf16[2048,128]{1,0:T(8,128)(2,1)} %bitcast.9, bf16[2048,128]{1,0:T(8,128)(2,1)} %bitcast.10, ...), custom_call_target="tpu_custom_call" | custom-call | tf_op jit(solution)/shard_map/layer/pallas_call | solution.py:394
  38.7 2.1 %settle.1 = (bf16[32,2048]{1,0:T(8,128)(2,1)}, bf16[2048,128]{1,0:T(8,128)(2,1)}, bf16[2048,128]{1,0:T(8,128)(2,1)}) custom-call(bf16[2,32,1024]{2,1,0:T(8,128)(2,1)} %get-tuple-element.9.half_h, bf16[2048,128]{1,0:T(8,128)(2,1)} %get-tuple-element.10.ki_h, bf16[2048,128]{1,0:T(8,128)(2,1)} %get-tuple-element.11.vi_h), custom_call_target="tpu_custom_call" | custom-call | tf_op jit(solution)/shard_map/settle/pallas_call | solution.py:345

commit v4 on v3

--- a/solution.py
+++ b/solution.py
@@ -47,7 +47,7 @@
                  x_v, pos_v, ids_v, kc_v, vc_v, gin_v, gres_v, gpost_v, wq_v, wk_v, wv_v, wo_v, wg_v, wu_v, wr_v,
                  eg_v, eu_v, ed_v, ko_v, vo_v, a_v, m_v, q_v, mix_v, as_v, ar_v, h_v, c_v, act_v, den_v,
                  ds_v, dr_v, dp_v, near_v, far_v, gu_v, z_v, xs_v, xr_v, own_v, rs_v, rr_v, ret_v, fs_v, fr_v, out_v,
-                 small_sem, w_sem, out_sem, tp_sem, ep_sem):
+                 small_sem, w_sem, ff_sem, out_sem, tp_sem, ep_sem):
     T, D, L, KV, HD, QH, F, EL, EF, EP, CAP, TILE = dims
     group = QH // KV
     slots = EP * CAP
@@ -63,13 +63,13 @@
     digit = [[lax.rem(p + d, side) * side ** (2 - axis) for d in range(side)] for axis, p in enumerate(at)]
     peers = [digit[0][i] + digit[1][j] + digit[2][k] for i, j, k in steps]
 
+    small = [(x_h, x_v), (ids_h, ids_v), (gpost_h, gpost_v), (gin_h, gin_v), (pos_h, pos_v), (gres_h, gres_v)]
+    for i, (src, dst) in enumerate(small):
+        pltpu.make_async_copy(src, dst, small_sem.at[i]).start()
+
     for peer in peers:
         pl.semaphore_signal(barrier, inc=1, device_id={'ep': peer}, device_id_type=MESH)
     pl.semaphore_signal(barrier, inc=1, device_id={'tp': other}, device_id_type=MESH)
-
-    small = [(x_h, x_v), (pos_h, pos_v), (ids_h, ids_v), (gin_h, gin_v), (gres_h, gres_v), (gpost_h, gpost_v)]
-    for i, (src, dst) in enumerate(small):
-        pltpu.make_async_copy(src, dst, small_sem.at[i]).start()
 
     def fetch(src, dst, sem, parts):
         step = dst.shape[0] // parts
@@ -80,19 +80,12 @@
     def arrive(dst, sem):
         pltpu.make_async_copy(dst, dst, sem).wait()
 
-    fetch(wr_h, wr_v, w_sem.at[0], 1)
+    for i, (src, dst) in enumerate(small):
+        pltpu.make_async_copy(src, dst, small_sem.at[i]).wait()
+
     fetch(wk_h, wk_v, w_sem.at[1], 1)
     fetch(wv_h, wv_v, w_sem.at[2], 1)
-    fetch(wq_h, wq_v, w_sem.at[3], 4)
-    fetch(kc_h, kc_v, w_sem.at[4], 1)
-    fetch(vc_h, vc_v, w_sem.at[5], 1)
-    fetch(wo_h, wo_v, w_sem.at[6], 4)
-    fetch(eg_h, eg_v, w_sem.at[7], EL)
-    fetch(eu_h, eu_v, w_sem.at[8], EL)
-    fetch(ed_h, ed_v, w_sem.at[9], EL)
-
-    for i, (src, dst) in enumerate(small):
-        pltpu.make_async_copy(src, dst, small_sem.at[i]).wait()
+    fetch(wq_h, wq_v, w_sem.at[3], 2)
 
     wide = x_v[...].astype(F32)
     scaled = wide * inv_rms(wide)
@@ -127,30 +120,11 @@
     ds_v[:, :, :HALF] = sent.reshape(EP, CAP, HALF)
     ds_v[:, :, HALF:] = jnp.broadcast_to(which, (slots, 128)).astype(BF16).reshape(EP, CAP, 128)
 
-    arrive(wr_v, w_sem.at[0])
-    logits = jnp.dot(moe_in, wr_v[...], preferred_element_type=F32)
-    expd = jnp.exp(logits - jnp.max(logits, axis=-1, keepdims=True))
-    probs = expd / jnp.sum(expd, axis=-1, keepdims=True)
-    lane = iota(logits.shape, 1).astype(F32)
-    picked = [jnp.sum(jnp.where(lane == to_col(r), probs, 0.0), axis=1, keepdims=True) for r in id_rows]
-    total = picked[0] + picked[1]
-    weights = [pk / total for pk in picked]
-
-    pl.semaphore_wait(barrier, EP)
-
-    def exchange(src, dst, sem):
-        for peer in peers:
-            pltpu.make_async_remote_copy(src_ref=src.at[peer], dst_ref=dst.at[me], send_sem=ep_sem.at[sem], recv_sem=ep_sem.at[sem + 1],
-                                         device_id={'ep': peer}, device_id_type=MESH).start()
-
-    exchange(ds_v, dr_v, 0)
-    dr_v[me] = ds_v[me]
-
-    def tiled(width, body, tile=TILE):
+    def tiled(width, body, tile=TILE, first=0):
         tile = min(tile, width)
 
         def step(i, carry):
-            body(pl.ds(pl.multiple_of(i * tile, tile), tile))
+            body(pl.ds(pl.multiple_of(first + i * tile, tile), tile))
             return carry
 
         lax.fori_loop(0, width // tile, step, 0)
@@ -170,14 +144,35 @@
     v_proj = jnp.dot(a_v[...], wv_v[...], preferred_element_type=F32).astype(BF16)
     v_new = jnp.concatenate([v_proj[:, g * HD:(g + 1) * HD] for g in range(KV)], axis=0)
 
+    fetch(kc_h, kc_v, w_sem.at[4], 1)
+    fetch(vc_h, vc_v, w_sem.at[5], 1)
+    fetch(wo_h, wo_v, w_sem.at[6], 2)
+
+    pl.semaphore_wait(barrier, EP)
+
+    def exchange(src, dst, sem):
+        for peer in peers:
+            pltpu.make_async_remote_copy(src_ref=src.at[peer], dst_ref=dst.at[me], send_sem=ep_sem.at[sem], recv_sem=ep_sem.at[sem + 1],
+                                         device_id={'ep': peer}, device_id_type=MESH).start()
+
+    exchange(ds_v, dr_v, 0)
+    dr_v[me] = ds_v[me]
+    fetch(eg_h, eg_v, w_sem.at[7], 1)
+    fetch(eu_h, eu_v, w_sem.at[8], 1)
+    fetch(ed_h, ed_v, w_sem.at[9], 1)
+    fetch(wr_h, wr_v, w_sem.at[0], 1)
+
     arrive(wq_v, w_sem.at[3])
 
     def q_tile(cols):
         q_v[:, cols] = jnp.dot(a_v[...], wq_v[:, cols], preferred_element_type=F32)
 
     tiled(QH * HD, q_tile)
-    fetch(wg_h, wg_v, w_sem.at[10], 4)
-    fetch(wu_h, wu_v, w_sem.at[11], 4)
+    blocks = 3 if F % (3 * TILE) == 0 else 1
+    ff_cols = [pl.ds(i * (F // blocks), F // blocks) for i in range(blocks)]
+    for i, cols in enumerate(ff_cols):
+        pltpu.make_async_copy(wg_h.at[:, cols], wg_v.at[:, cols], ff_sem.at[2 * i]).start()
+        pltpu.make_async_copy(wu_h.at[:, cols], wu_v.at[:, cols], ff_sem.at[2 * i + 1]).start()
     half = min(wd_h.shape[0], wq_v.shape[0])
     rest = wd_h.shape[0] - half
     pltpu.make_async_copy(wd_h.at[pl.ds(0, half)], wq_v.at[pl.ds(0, half)], w_sem.at[12]).start()
@@ -229,11 +224,6 @@
     attn_copy = pltpu.make_async_remote_copy(src_ref=as_v, dst_ref=ar_v, send_sem=tp_sem.at[0], recv_sem=tp_sem.at[1],
                                              device_id={'tp': other}, device_id_type=MESH)
     attn_copy.start()
-    attn_copy.wait()
-    mid = (x_v[...].astype(F32) + (as_v[...].astype(F32) + ar_v[...].astype(F32))).astype(BF16)
-    h_v[...] = mid
-    mid = mid.astype(F32)
-    c_v[...] = (mid * inv_rms(mid) * gain_row(gres_v)).astype(BF16)
 
     arrive(eg_v, w_sem.at[7])
     arrive(eu_v, w_sem.at[8])
@@ -266,20 +256,25 @@
                                             device_id={'tp': other}, device_id_type=MESH)
     sum_copy.start()
     own_v[...] = expert_down(mine_half)
+    attn_copy.wait()
+    mid = (x_v[...].astype(F32) + (as_v[...].astype(F32) + ar_v[...].astype(F32))).astype(BF16)
+    h_v[...] = mid
+    mid = mid.astype(F32)
+    c_v[...] = (mid * inv_rms(mid) * gain_row(gres_v)).astype(BF16)
     sum_copy.wait()
     rs_v[...] = (own_v[...] + xr_v[...].astype(F32)).astype(BF16).reshape(EP, CAP, HALF)
     exchange(rs_v, rr_v, 2)
     rr_v[me] = rs_v[me]
 
-    arrive(wg_v, w_sem.at[10])
-    arrive(wu_v, w_sem.at[11])
-
     def ff_tile(cols):
         gate = jnp.dot(c_v[...], wg_v[:, cols], preferred_element_type=F32)
         up = jnp.dot(c_v[...], wu_v[:, cols], preferred_element_type=F32)
         act_v[:, cols] = silu_mul(gate, up)
 
-    tiled(F, ff_tile)
+    for i, cols in enumerate(ff_cols):
+        arrive(wg_v.at[:, cols], ff_sem.at[2 * i])
+        arrive(wu_v.at[:, cols], ff_sem.at[2 * i + 1])
+        tiled(F // blocks, ff_tile, first=i * (F // blocks))
 
     arrive(wq_v.at[pl.ds(0, half)], w_sem.at[12])
     if rest:
@@ -298,6 +293,14 @@
     dense_copy.start()
     dense_copy.wait()
     den_v[...] = h_v[:, mine_half].astype(F32) + (fs_v[:, mine_half].astype(F32) + fr_v[:, mine_half].astype(F32))
+    arrive(wr_v, w_sem.at[0])
+    logits = jnp.dot(m_v[...], wr_v[...], preferred_element_type=F32)
+    expd = jnp.exp(logits - jnp.max(logits, axis=-1, keepdims=True))
+    probs = expd / jnp.sum(expd, axis=-1, keepdims=True)
+    lane = iota(logits.shape, 1).astype(F32)
+    picked = [jnp.sum(jnp.where(lane == to_col(r), probs, 0.0), axis=1, keepdims=True) for r in id_rows]
+    total = picked[0] + picked[1]
+    weights = [pk / total for pk in picked]
     slot_lane = iota((T, slots), 1).astype(F32)
     take = [jnp.where(slot_lane == s, 1.0, 0.0).astype(BF16) for s in slot_cols]
 
@@ -387,7 +390,7 @@
             pltpu.VMEM((slots, EL * EF), BF16), pltpu.VMEM((slots, HALF), BF16), pltpu.VMEM((slots, HALF), BF16), pltpu.VMEM((slots, HALF), F32),
             pltpu.VMEM((EP, CAP, HALF), BF16), pltpu.VMEM((EP, CAP, HALF), BF16), pltpu.VMEM((slots, HALF), BF16),
             pltpu.VMEM((T, D), BF16), pltpu.VMEM((T, D), BF16), pltpu.VMEM((T, HALF), BF16),
-            pltpu.SemaphoreType.DMA((6,)), pltpu.SemaphoreType.DMA((14,)), pltpu.SemaphoreType.DMA((3,)),
+            pltpu.SemaphoreType.DMA((6,)), pltpu.SemaphoreType.DMA((14,)), pltpu.SemaphoreType.DMA((6,)), pltpu.SemaphoreType.DMA((3,)),
             pltpu.SemaphoreType.DMA((10,)), pltpu.SemaphoreType.DMA((4,)),
         ]
         hbm = pl.BlockSpec(memory_space=pl.ANY)

time: 40.9 us -> 35.2 us (0.86)
  Pallas kernels: 40.2 us -> 34.4 us
    pallas_call x1, Pallas kernels: 38.1 us -> 32.3 us  [local_layer(): pl.pallas_call(functools.partial(layer_kernel, dims), out_shape=(jax.Shap...]
where the time goes in v4:
time: 35.2 us; the launch traced here: 35 us
  Pallas kernels  34.4 us (98%)
  between operations  0.65 us (2%)
    pallas_call x1, Pallas kernels, local_layer(): pl.pallas_call(functools.partial(layer_kernel, dims), out_shape=(jax.Shap...  32.3 us
    pallas_call x1, Pallas kernels, settle(): pl.pallas_call(settle_kernel, out_shape=tuple((jax.ShapeDtypeStruct(s, BF...  2.1 us

profile of v4, /device:TPU:1, one launch (start us, length us, event | category | flops | bytes accessed | tf_op | source)
XLA Modules:
  0.0 35.0 jit_solution(15586637807566764735)
XLA Ops:
  0.6 32.3 %layer.1 = (bf16[2,32,1024]{2,1,0:T(8,128)(2,1)}, bf16[2048,128]{1,0:T(8,128)(2,1)}, bf16[2048,128]{1,0:T(8,128)(2,1)}) custom-call(bf16[32,2048]{1,0:T(8,128)(2,1)} %x_h.1, s32[1,32]{1,0:T(1,128)} %bitcast.15, s32[2,32]{1,0:T(2,128)} %bitcast.14, bf16[2048,128]{1,0:T(8,128)(2,1)} %bitcast.9, bf16[2048,128]{1,0:T(8,128)(2,1)} %bitcast.10, ...), custom_call_target="tpu_custom_call" | custom-call | tf_op jit(solution)/shard_map/layer/pallas_call | solution.py:397
  32.9 2.1 %settle.1 = (bf16[32,2048]{1,0:T(8,128)(2,1)}, bf16[2048,128]{1,0:T(8,128)(2,1)}, bf16[2048,128]{1,0:T(8,128)(2,1)}) custom-call(bf16[2,32,1024]{2,1,0:T(8,128)(2,1)} %get-tuple-element.9.half_h, bf16[2048,128]{1,0:T(8,128)(2,1)} %get-tuple-element.10.ki_h, bf16[2048,128]{1,0:T(8,128)(2,1)} %get-tuple-element.11.vi_h), custom_call_target="tpu_custom_call" | custom-call | tf_op jit(solution)/shard_map/settle/pallas_call | solution.py:348

commit v5 on v4

--- a/solution.py
+++ b/solution.py
@@ -67,10 +67,6 @@
     for i, (src, dst) in enumerate(small):
         pltpu.make_async_copy(src, dst, small_sem.at[i]).start()
 
-    for peer in peers:
-        pl.semaphore_signal(barrier, inc=1, device_id={'ep': peer}, device_id_type=MESH)
-    pl.semaphore_signal(barrier, inc=1, device_id={'tp': other}, device_id_type=MESH)
-
     def fetch(src, dst, sem, parts):
         step = dst.shape[0] // parts
         for i in range(parts):
@@ -80,11 +76,16 @@
     def arrive(dst, sem):
         pltpu.make_async_copy(dst, dst, sem).wait()
 
+    fetch(wk_h, wk_v, w_sem.at[1], 1)
+    fetch(wv_h, wv_v, w_sem.at[2], 1)
+
+    for peer in peers:
+        pl.semaphore_signal(barrier, inc=1, device_id={'ep': peer}, device_id_type=MESH)
+    pl.semaphore_signal(barrier, inc=1, device_id={'tp': other}, device_id_type=MESH)
+
     for i, (src, dst) in enumerate(small):
         pltpu.make_async_copy(src, dst, small_sem.at[i]).wait()
 
-    fetch(wk_h, wk_v, w_sem.at[1], 1)
-    fetch(wv_h, wv_v, w_sem.at[2], 1)
     fetch(wq_h, wq_v, w_sem.at[3], 2)
 
     wide = x_v[...].astype(F32)
@@ -120,15 +121,6 @@
     ds_v[:, :, :HALF] = sent.reshape(EP, CAP, HALF)
     ds_v[:, :, HALF:] = jnp.broadcast_to(which, (slots, 128)).astype(BF16).reshape(EP, CAP, 128)
 
-    def tiled(width, body, tile=TILE, first=0):
-        tile = min(tile, width)
-
-        def step(i, carry):
-            body(pl.ds(pl.multiple_of(first + i * tile, tile), tile))
-            return carry
-
-        lax.fori_loop(0, width // tile, step, 0)
-
     inv_freq = jnp.exp((iota((1, HD), 1) & (HD // 2 - 1)).astype(F32) * (-2.0 / HD * math.log(ROPE_BASE)))
     angles = pos_col * inv_freq
     cosine = jnp.cos(angles)
@@ -164,10 +156,7 @@
 
     arrive(wq_v, w_sem.at[3])
 
-    def q_tile(cols):
-        q_v[:, cols] = jnp.dot(a_v[...], wq_v[:, cols], preferred_element_type=F32)
-
-    tiled(QH * HD, q_tile)
+    q_v[...] = jnp.dot(a_v[...], wq_v[...], preferred_element_type=F32)
     blocks = 3 if F % (3 * TILE) == 0 else 1
     ff_cols = [pl.ds(i * (F // blocks), F // blocks) for i in range(blocks)]
     for i, cols in enumerate(ff_cols):
@@ -198,27 +187,34 @@
         vo_v[rows, :] = v_all
         q_rows = jnp.concatenate([q[c * TC:(c + 1) * TC] for q in q_heads], axis=0)
         scores = lax.dot_general(q_rows, k_all, (((1,), (1,)), ((), ())), preferred_element_type=F32) * (HD ** -0.5)
-        head_kv = iota((QH * TC, 1), 0) // (group * TC)
-        base = lax.rem(iota((QH * TC, 1), 0), TC) * (L * KV) + head_kv
+        base = lax.rem(iota((QH * TC, 1), 0), TC) * (L * KV)
         pos_rows = jnp.concatenate([pos_col[c * TC:(c + 1) * TC]] * QH, axis=0).astype(jnp.int32)
-        last = base + KV * pos_rows
-        col = iota((QH * TC, width), 1)
-        visible = (col >= base) & (col <= last) & (lax.rem(col, KV) == head_kv)
-        scores = jnp.where(visible, scores, -jnp.inf)
-        expo = jnp.exp(scores - jnp.max(scores, axis=-1, keepdims=True))
-        attn = (expo / jnp.sum(expo, axis=-1, keepdims=True)).astype(BF16)
+        last = base + KV * pos_rows + (KV - 1)
+        col = iota((1, width), 1)
+        attn = []
+        for g in range(KV):
+            part = slice(g * group * TC, (g + 1) * group * TC)
+            own_col = jnp.where(lax.rem(col, KV) == g, col, -1)
+            visible = (own_col >= base[part]) & (own_col <= last[part])
+            sub = jnp.where(visible, scores[part], -jnp.inf)
+            expo = jnp.exp(sub - jnp.max(sub, axis=-1, keepdims=True))
+            attn.append((expo * (1.0 / jnp.sum(expo, axis=-1, keepdims=True))).astype(BF16))
+        attn = jnp.concatenate(attn, axis=0)
         mixed = jnp.dot(attn, v_all, preferred_element_type=F32).astype(BF16)
         mix_v[c * TC:(c + 1) * TC, :] = jnp.concatenate([mixed[h * TC:(h + 1) * TC] for h in range(QH)], axis=1)
     cache_out = [pltpu.make_async_copy(ko_v, ko_h, out_sem.at[0]), pltpu.make_async_copy(vo_v, vo_h, out_sem.at[1])]
     for copy in cache_out:
         copy.start()
 
+    others = pl.ds(0, EP - 1)
+    pltpu.make_async_copy(dr_v.at[others], dr_v.at[others], ep_sem.at[1]).wait()
+    rows_copy = pltpu.make_async_remote_copy(src_ref=dr_v, dst_ref=dp_v, send_sem=tp_sem.at[4], recv_sem=tp_sem.at[5],
+                                             device_id={'tp': other}, device_id_type=MESH)
+    rows_copy.start()
+
     arrive(wo_v, w_sem.at[6])
 
-    def o_tile(cols):
-        as_v[:, cols] = jnp.dot(mix_v[...], wo_v[:, cols], preferred_element_type=F32).astype(BF16)
-
-    tiled(D, o_tile)
+    as_v[...] = jnp.dot(mix_v[...], wo_v[...], preferred_element_type=F32).astype(BF16)
     if rest:
         pltpu.make_async_copy(wd_h.at[pl.ds(half, rest)], wo_v.at[pl.ds(0, rest)], w_sem.at[13]).start()
     attn_copy = pltpu.make_async_remote_copy(src_ref=as_v, dst_ref=ar_v, send_sem=tp_sem.at[0], recv_sem=tp_sem.at[1],
@@ -227,11 +223,6 @@
 
     arrive(eg_v, w_sem.at[7])
     arrive(eu_v, w_sem.at[8])
-    others = pl.ds(0, EP - 1)
-    pltpu.make_async_copy(dr_v.at[others], dr_v.at[others], ep_sem.at[1]).wait()
-    rows_copy = pltpu.make_async_remote_copy(src_ref=dr_v, dst_ref=dp_v, send_sem=tp_sem.at[4], recv_sem=tp_sem.at[5],
-                                             device_id={'tp': other}, device_id_type=MESH)
-    rows_copy.start()
     near_v[...] = dr_v[...].reshape(slots, HALF + 128)
     for e in range(EL):
         gu_v[2 * e] = jnp.dot(near_v[:, :HALF], eg_v[e, mine_half, :], preferred_element_type=F32)
@@ -261,38 +252,6 @@
     h_v[...] = mid
     mid = mid.astype(F32)
     c_v[...] = (mid * inv_rms(mid) * gain_row(gres_v)).astype(BF16)
-    sum_copy.wait()
-    rs_v[...] = (own_v[...] + xr_v[...].astype(F32)).astype(BF16).reshape(EP, CAP, HALF)
-    exchange(rs_v, rr_v, 2)
-    rr_v[me] = rs_v[me]
-
-    def ff_tile(cols):
-        gate = jnp.dot(c_v[...], wg_v[:, cols], preferred_element_type=F32)
-        up = jnp.dot(c_v[...], wu_v[:, cols], preferred_element_type=F32)
-        act_v[:, cols] = silu_mul(gate, up)
-
-    for i, cols in enumerate(ff_cols):
-        arrive(wg_v.at[:, cols], ff_sem.at[2 * i])
-        arrive(wu_v.at[:, cols], ff_sem.at[2 * i + 1])
-        tiled(F // blocks, ff_tile, first=i * (F // blocks))
-
-    arrive(wq_v.at[pl.ds(0, half)], w_sem.at[12])
-    if rest:
-        arrive(wo_v.at[pl.ds(0, rest)], w_sem.at[13])
-
-    def down_tile(cols):
-        part = jnp.dot(act_v[:, :half], wq_v[:half, cols], preferred_element_type=F32)
-        if rest:
-            part += jnp.dot(act_v[:, half:], wo_v[:rest, cols], preferred_element_type=F32)
-        fs_v[:, cols] = part.astype(BF16)
-
-    tiled(D, down_tile)
-
-    dense_copy = pltpu.make_async_remote_copy(src_ref=fs_v, dst_ref=fr_v, send_sem=tp_sem.at[2], recv_sem=tp_sem.at[3],
-                                              device_id={'tp': other}, device_id_type=MESH)
-    dense_copy.start()
-    dense_copy.wait()
-    den_v[...] = h_v[:, mine_half].astype(F32) + (fs_v[:, mine_half].astype(F32) + fr_v[:, mine_half].astype(F32))
     arrive(wr_v, w_sem.at[0])
     logits = jnp.dot(m_v[...], wr_v[...], preferred_element_type=F32)
     expd = jnp.exp(logits - jnp.max(logits, axis=-1, keepdims=True))
@@ -304,11 +263,40 @@
     slot_lane = iota((T, slots), 1).astype(F32)
     take = [jnp.where(slot_lane == s, 1.0, 0.0).astype(BF16) for s in slot_cols]
 
+    sum_copy.wait()
+    rs_v[...] = (own_v[...] + xr_v[...].astype(F32)).astype(BF16).reshape(EP, CAP, HALF)
+    exchange(rs_v, rr_v, 2)
+    rr_v[me] = rs_v[me]
+
+    for i, cols in enumerate(ff_cols):
+        arrive(wg_v.at[:, cols], ff_sem.at[2 * i])
+        arrive(wu_v.at[:, cols], ff_sem.at[2 * i + 1])
+        gate = jnp.dot(c_v[...], wg_v[:, cols], preferred_element_type=F32)
+        up = jnp.dot(c_v[...], wu_v[:, cols], preferred_element_type=F32)
+        act_v[:, cols] = silu_mul(gate, up)
+
+    arrive(wq_v.at[pl.ds(0, half)], w_sem.at[12])
+    if rest:
+        arrive(wo_v.at[pl.ds(0, rest)], w_sem.at[13])
+
+    def down(cols):
+        part = jnp.dot(act_v[:, :half], wq_v[:half, cols], preferred_element_type=F32)
+        if rest:
+            part += jnp.dot(act_v[:, half:], wo_v[:rest, cols], preferred_element_type=F32)
+        return part
+
+    fs_v[...] = down(other_half).astype(BF16)
+    dense_copy = pltpu.make_async_remote_copy(src_ref=fs_v, dst_ref=fr_v, send_sem=tp_sem.at[2], recv_sem=tp_sem.at[3],
+                                              device_id={'tp': other}, device_id_type=MESH)
+    dense_copy.start()
+    den_v[...] = h_v[:, mine_half].astype(F32) + down(mine_half)
+
     pltpu.make_async_copy(rr_v.at[others], rr_v.at[others], ep_sem.at[3]).wait()
     ret_v[...] = rr_v[...].reshape(slots, HALF)
     moe = weights[0] * jnp.dot(take[0], ret_v[...], preferred_element_type=F32)
     moe += weights[1] * jnp.dot(take[1], ret_v[...], preferred_element_type=F32)
-    out_v[...] = (den_v[...] + moe).astype(BF16)
+    dense_copy.wait()
+    out_v[...] = (den_v[...] + fr_v[...].astype(F32) + moe).astype(BF16)
     last_copy = pltpu.make_async_remote_copy(src_ref=out_v, dst_ref=out_h.at[mine], send_sem=tp_sem.at[8], recv_sem=tp_sem.at[9],
                                              device_id={'tp': other}, device_id_type=MESH)
     last_copy.start()
@@ -389,7 +377,7 @@
             pltpu.VMEM((slots, HALF + 128), BF16), pltpu.VMEM((slots, HALF), BF16), pltpu.VMEM((2 * EL, slots, EF), F32),
             pltpu.VMEM((slots, EL * EF), BF16), pltpu.VMEM((slots, HALF), BF16), pltpu.VMEM((slots, HALF), BF16), pltpu.VMEM((slots, HALF), F32),
             pltpu.VMEM((EP, CAP, HALF), BF16), pltpu.VMEM((EP, CAP, HALF), BF16), pltpu.VMEM((slots, HALF), BF16),
-            pltpu.VMEM((T, D), BF16), pltpu.VMEM((T, D), BF16), pltpu.VMEM((T, HALF), BF16),
+            pltpu.VMEM((T, HALF), BF16), pltpu.VMEM((T, HALF), BF16), pltpu.VMEM((T, HALF), BF16),
             pltpu.SemaphoreType.DMA((6,)), pltpu.SemaphoreType.DMA((14,)), pltpu.SemaphoreType.DMA((6,)), pltpu.SemaphoreType.DMA((3,)),
             pltpu.SemaphoreType.DMA((10,)), pltpu.SemaphoreType.DMA((4,)),
         ]

time: 35.2 us -> 33.4 us (0.949)
  Pallas kernels: 34.4 us -> 32.6 us
    pallas_call x1, Pallas kernels: 32.3 us -> 30.5 us  [local_layer(): pl.pallas_call(functools.partial(layer_kernel, dims), out_shape=(jax.Shap...]
where the time goes in v5:
time: 33.4 us; the launch traced here: 33.2 us
  Pallas kernels  32.6 us (98%)
  between operations  0.65 us (2%)
    pallas_call x1, Pallas kernels, local_layer(): pl.pallas_call(functools.partial(layer_kernel, dims), out_shape=(jax.Shap...  30.5 us
    pallas_call x1, Pallas kernels, settle(): pl.pallas_call(settle_kernel, out_shape=tuple((jax.ShapeDtypeStruct(s, BF...  2.1 us

profile of v5, /device:TPU:1, one launch (start us, length us, event | category | flops | bytes accessed | tf_op | source)
XLA Modules:
  0.0 33.2 jit_solution(13883595713051717088)
XLA Ops:
  0.6 30.5 %layer.1 = (bf16[2,32,1024]{2,1,0:T(8,128)(2,1)}, bf16[2048,128]{1,0:T(8,128)(2,1)}, bf16[2048,128]{1,0:T(8,128)(2,1)}) custom-call(bf16[32,2048]{1,0:T(8,128)(2,1)} %x_h.1, s32[1,32]{1,0:T(1,128)} %bitcast.15, s32[2,32]{1,0:T(2,128)} %bitcast.14, bf16[2048,128]{1,0:T(8,128)(2,1)} %bitcast.9, bf16[2048,128]{1,0:T(8,128)(2,1)} %bitcast.10, ...), custom_call_target="tpu_custom_call" | custom-call | tf_op jit(solution)/shard_map/layer/pallas_call | solution.py:385
  31.1 2.1 %settle.1 = (bf16[32,2048]{1,0:T(8,128)(2,1)}, bf16[2048,128]{1,0:T(8,128)(2,1)}, bf16[2048,128]{1,0:T(8,128)(2,1)}) custom-call(bf16[2,32,1024]{2,1,0:T(8,128)(2,1)} %get-tuple-element.9.half_h, bf16[2048,128]{1,0:T(8,128)(2,1)} %get-tuple-element.10.ki_h, bf16[2048,128]{1,0:T(8,128)(2,1)} %get-tuple-element.11.vi_h), custom_call_target="tpu_custom_call" | custom-call | tf_op jit(solution)/shard_map/settle/pallas_call | solution.py:336

commit v6 on v5

--- a/solution.py
+++ b/solution.py
@@ -27,6 +27,16 @@
     steps = [(a, b, c) for a in range(side) for b in range(side) for c in range(side)][1:]
     random.Random(1).shuffle(steps)
     return side, sorted(steps, key=lambda s: -sum(min(d, side - d) for d in s))
+
+
+def entry_level(at, side):
+    if side != 4:
+        return 0 * at[2]
+    cost = 0
+    for place, table in zip(at, ((0, 8, 17, 23), (0, 5, 10, 13), (0, 4, 9, 11))):
+        for i in range(1, 4):
+            cost = cost + jnp.where(place == i, table[i], 0)
+    return jnp.where(cost <= 12, 2, jnp.where(cost <= 22, 1, 0))
 
 
 def gain_row(ref):
@@ -140,6 +150,68 @@
     fetch(vc_h, vc_v, w_sem.at[5], 1)
     fetch(wo_h, wo_v, w_sem.at[6], 2)
 
+    blocks = 3 if F % (3 * TILE) == 0 else 1
+    ff_cols = [pl.ds(i * (F // blocks), F // blocks) for i in range(blocks)]
+    half = min(wd_h.shape[0], wq_v.shape[0])
+    rest = wd_h.shape[0] - half
+    cache_out = [pltpu.make_async_copy(ko_v, ko_h, out_sem.at[0]), pltpu.make_async_copy(vo_v, vo_h, out_sem.at[1])]
+    level = entry_level(at, side)
+
+    def queries():
+        arrive(wq_v, w_sem.at[3])
+        fetch(eg_h, eg_v, w_sem.at[7], 1)
+        fetch(eu_h, eu_v, w_sem.at[8], 1)
+        fetch(ed_h, ed_v, w_sem.at[9], 1)
+        fetch(wr_h, wr_v, w_sem.at[0], 1)
+        q_v[...] = jnp.dot(a_v[...], wq_v[...], preferred_element_type=F32)
+        for i, cols in enumerate(ff_cols):
+            pltpu.make_async_copy(wg_h.at[:, cols], wg_v.at[:, cols], ff_sem.at[2 * i]).start()
+            pltpu.make_async_copy(wu_h.at[:, cols], wu_v.at[:, cols], ff_sem.at[2 * i + 1]).start()
+        pltpu.make_async_copy(wd_h.at[pl.ds(0, half)], wq_v.at[pl.ds(0, half)], w_sem.at[12]).start()
+
+    def attention():
+        arrive(kc_v, w_sem.at[4])
+        arrive(vc_v, w_sem.at[5])
+        tok_i = iota((T, KV * T), 0)
+        lane_j = iota((T, KV * T), 1)
+        target = jnp.sum(jnp.where(lax.rem(lane_j, T) == tok_i, (tok_i.astype(F32) * L + pos_col) * KV, 0.0), axis=0, keepdims=True)
+        target = target + jnp.floor(iota((1, KV * T), 1).astype(F32) * (1.0 / T))
+        new_rows = jnp.concatenate([k_new, v_new, jnp.ones((KV * T, HD), BF16)], axis=1)
+        q_heads = [rope(q_v[:, h * HD:(h + 1) * HD]) for h in range(QH)]
+        TC = min(16, T)
+        width = TC * L * KV
+        for c in range(T // TC):
+            rows = pl.ds(c * width, width)
+            place = jnp.where(iota((width, KV * T), 0).astype(F32) + float(c * width) == target, 1.0, 0.0).astype(BF16)
+            placed = jnp.dot(place, new_rows, preferred_element_type=F32)
+            hit = placed[:, 2 * HD:] > 0.5
+            k_all = jnp.where(hit, placed[:, :HD], kc_v[rows, :].astype(F32)).astype(BF16)
+            v_all = jnp.where(hit, placed[:, HD:2 * HD], vc_v[rows, :].astype(F32)).astype(BF16)
+            ko_v[rows, :] = k_all
+            vo_v[rows, :] = v_all
+            q_rows = jnp.concatenate([q[c * TC:(c + 1) * TC] for q in q_heads], axis=0)
+            scores = lax.dot_general(q_rows, k_all, (((1,), (1,)), ((), ())), preferred_element_type=F32) * (HD ** -0.5)
+            base = lax.rem(iota((QH * TC, 1), 0), TC) * (L * KV)
+            pos_rows = jnp.concatenate([pos_col[c * TC:(c + 1) * TC]] * QH, axis=0).astype(jnp.int32)
+            last = base + KV * pos_rows + (KV - 1)
+            col = iota((1, width), 1)
+            attn = []
+            for g in range(KV):
+                part = slice(g * group * TC, (g + 1) * group * TC)
+                own_col = jnp.where(lax.rem(col, KV) == g, col, -1)
+                visible = (own_col >= base[part]) & (own_col <= last[part])
+                sub = jnp.where(visible, scores[part], -jnp.inf)
+                expo = jnp.exp(sub - jnp.max(sub, axis=-1, keepdims=True))
+                attn.append((expo * (1.0 / jnp.sum(expo, axis=-1, keepdims=True))).astype(BF16))
+            attn = jnp.concatenate(attn, axis=0)
+            mixed = jnp.dot(attn, v_all, preferred_element_type=F32).astype(BF16)
+            mix_v[c * TC:(c + 1) * TC, :] = jnp.concatenate([mixed[h * TC:(h + 1) * TC] for h in range(QH)], axis=1)
+        for copy in cache_out:
+            copy.start()
+
+    pl.when(level >= 1)(queries)
+    pl.when(level >= 2)(attention)
+
     pl.semaphore_wait(barrier, EP)
 
     def exchange(src, dst, sem):
@@ -149,62 +221,23 @@
 
     exchange(ds_v, dr_v, 0)
     dr_v[me] = ds_v[me]
-    fetch(eg_h, eg_v, w_sem.at[7], 1)
-    fetch(eu_h, eu_v, w_sem.at[8], 1)
-    fetch(ed_h, ed_v, w_sem.at[9], 1)
-    fetch(wr_h, wr_v, w_sem.at[0], 1)
-
-    arrive(wq_v, w_sem.at[3])
-
-    q_v[...] = jnp.dot(a_v[...], wq_v[...], preferred_element_type=F32)
-    blocks = 3 if F % (3 * TILE) == 0 else 1
-    ff_cols = [pl.ds(i * (F // blocks), F // blocks) for i in range(blocks)]
-    for i, cols in enumerate(ff_cols):
-        pltpu.make_async_copy(wg_h.at[:, cols], wg_v.at[:, cols], ff_sem.at[2 * i]).start()
-        pltpu.make_async_copy(wu_h.at[:, cols], wu_v.at[:, cols], ff_sem.at[2 * i + 1]).start()
-    half = min(wd_h.shape[0], wq_v.shape[0])
-    rest = wd_h.shape[0] - half
-    pltpu.make_async_copy(wd_h.at[pl.ds(0, half)], wq_v.at[pl.ds(0, half)], w_sem.at[12]).start()
-
-    arrive(kc_v, w_sem.at[4])
-    arrive(vc_v, w_sem.at[5])
-    tok_i = iota((T, KV * T), 0)
-    lane_j = iota((T, KV * T), 1)
-    target = jnp.sum(jnp.where(lax.rem(lane_j, T) == tok_i, (tok_i.astype(F32) * L + pos_col) * KV, 0.0), axis=0, keepdims=True)
-    target = target + jnp.floor(iota((1, KV * T), 1).astype(F32) * (1.0 / T))
-    new_rows = jnp.concatenate([k_new, v_new, jnp.ones((KV * T, HD), BF16)], axis=1)
-    q_heads = [rope(q_v[:, h * HD:(h + 1) * HD]) for h in range(QH)]
-    TC = min(16, T)
-    width = TC * L * KV
-    for c in range(T // TC):
-        rows = pl.ds(c * width, width)
-        place = jnp.where(iota((width, KV * T), 0).astype(F32) + float(c * width) == target, 1.0, 0.0).astype(BF16)
-        placed = jnp.dot(place, new_rows, preferred_element_type=F32)
-        hit = placed[:, 2 * HD:] > 0.5
-        k_all = jnp.where(hit, placed[:, :HD], kc_v[rows, :].astype(F32)).astype(BF16)
-        v_all = jnp.where(hit, placed[:, HD:2 * HD], vc_v[rows, :].astype(F32)).astype(BF16)
-        ko_v[rows, :] = k_all
-        vo_v[rows, :] = v_all
-        q_rows = jnp.concatenate([q[c * TC:(c + 1) * TC] for q in q_heads], axis=0)
-        scores = lax.dot_general(q_rows, k_all, (((1,), (1,)), ((), ())), preferred_element_type=F32) * (HD ** -0.5)
-        base = lax.rem(iota((QH * TC, 1), 0), TC) * (L * KV)
-        pos_rows = jnp.concatenate([pos_col[c * TC:(c + 1) * TC]] * QH, axis=0).astype(jnp.int32)
-        last = base + KV * pos_rows + (KV - 1)
-        col = iota((1, width), 1)
-        attn = []
-        for g in range(KV):
-            part = slice(g * group * TC, (g + 1) * group * TC)
-            own_col = jnp.where(lax.rem(col, KV) == g, col, -1)
-            visible = (own_col >= base[part]) & (own_col <= last[part])
-            sub = jnp.where(visible, scores[part], -jnp.inf)
-            expo = jnp.exp(sub - jnp.max(sub, axis=-1, keepdims=True))
-            attn.append((expo * (1.0 / jnp.sum(expo, axis=-1, keepdims=True))).astype(BF16))
-        attn = jnp.concatenate(attn, axis=0)
-        mixed = jnp.dot(attn, v_all, preferred_element_type=F32).astype(BF16)
-        mix_v[c * TC:(c + 1) * TC, :] = jnp.concatenate([mixed[h * TC:(h + 1) * TC] for h in range(QH)], axis=1)
-    cache_out = [pltpu.make_async_copy(ko_v, ko_h, out_sem.at[0]), pltpu.make_async_copy(vo_v, vo_h, out_sem.at[1])]
-    for copy in cache_out:
-        copy.start()
+
+    pl.when(level < 1)(queries)
+    pl.when(level < 2)(attention)
+
+
+    attn_copy = pltpu.make_async_remote_copy(src_ref=as_v, dst_ref=ar_v, send_sem=tp_sem.at[0], recv_sem=tp_sem.at[1],
+                                             device_id={'tp': other}, device_id_type=MESH)
+
+    def project():
+        arrive(wo_v, w_sem.at[6])
+
+        as_v[...] = jnp.dot(mix_v[...], wo_v[...], preferred_element_type=F32).astype(BF16)
+        if rest:
+            pltpu.make_async_copy(wd_h.at[pl.ds(half, rest)], wo_v.at[pl.ds(0, rest)], w_sem.at[13]).start()
+        attn_copy.start()
+
+    pl.when(level >= 2)(project)
 
     others = pl.ds(0, EP - 1)
     pltpu.make_async_copy(dr_v.at[others], dr_v.at[others], ep_sem.at[1]).wait()
@@ -212,14 +245,7 @@
                                              device_id={'tp': other}, device_id_type=MESH)
     rows_copy.start()
 
-    arrive(wo_v, w_sem.at[6])
-
-    as_v[...] = jnp.dot(mix_v[...], wo_v[...], preferred_element_type=F32).astype(BF16)
-    if rest:
-        pltpu.make_async_copy(wd_h.at[pl.ds(half, rest)], wo_v.at[pl.ds(0, rest)], w_sem.at[13]).start()
-    attn_copy = pltpu.make_async_remote_copy(src_ref=as_v, dst_ref=ar_v, send_sem=tp_sem.at[0], recv_sem=tp_sem.at[1],
-                                             device_id={'tp': other}, device_id_type=MESH)
-    attn_copy.start()
+    pl.when(level < 2)(project)
 
     arrive(eg_v, w_sem.at[7])
     arrive(eu_v, w_sem.at[8])

time: 33.4 us -> 34.9 us (1.045)
  Pallas kernels: 32.6 us -> 34 us
    pallas_call x1, Pallas kernels: 30.5 us -> 31.9 us  [local_layer(): pl.pallas_call(functools.partial(layer_kernel, dims), out_shape=(jax.Shap...]
where the time goes in v6:
time: 34.9 us; the launch traced here: 34.8 us
  Pallas kernels  34 us (97%)
  between operations  0.81 us (2%)
    pallas_call x1, Pallas kernels, local_layer(): pl.pallas_call(functools.partial(layer_kernel, dims), out_shape=(jax.Shap...  31.9 us
    pallas_call x1, Pallas kernels, settle(): pl.pallas_call(settle_kernel, out_shape=tuple((jax.ShapeDtypeStruct(s, BF...  2.1 us

profile of v6, /device:TPU:1, one launch (start us, length us, event | category | flops | bytes accessed | tf_op | source)
XLA Modules:
  0.0 34.8 jit_solution(7344242166406568077)
XLA Ops:
  0.6 31.9 %layer.1 = (bf16[2,32,1024]{2,1,0:T(8,128)(2,1)}, bf16[2048,128]{1,0:T(8,128)(2,1)}, bf16[2048,128]{1,0:T(8,128)(2,1)}) custom-call(bf16[32,2048]{1,0:T(8,128)(2,1)} %x_h.1, s32[1,32]{1,0:T(1,128)} %bitcast.15, s32[2,32]{1,0:T(2,128)} %bitcast.14, bf16[2048,128]{1,0:T(8,128)(2,1)} %bitcast.9, bf16[2048,128]{1,0:T(8,128)(2,1)} %bitcast.10, ...), custom_call_target="tpu_custom_call" | custom-call | tf_op jit(solution)/shard_map/layer/pallas_call | solution.py:411
  32.5 2.1 %settle.1 = (bf16[32,2048]{1,0:T(8,128)(2,1)}, bf16[2048,128]{1,0:T(8,128)(2,1)}, bf16[2048,128]{1,0:T(8,128)(2,1)}) custom-call(bf16[2,32,1024]{2,1,0:T(8,128)(2,1)} %get-tuple-element.9.half_h, bf16[2048,128]{1,0:T(8,128)(2,1)} %get-tuple-element.10.ki_h, bf16[2048,128]{1,0:T(8,128)(2,1)} %get-tuple-element.11.vi_h), custom_call_target="tpu_custom_call" | custom-call | tf_op jit(solution)/shard_map/settle/pallas_call | solution.py:362

commit v7 on v5

--- a/solution.py
+++ b/solution.py
@@ -27,6 +27,16 @@
     steps = [(a, b, c) for a in range(side) for b in range(side) for c in range(side)][1:]
     random.Random(1).shuffle(steps)
     return side, sorted(steps, key=lambda s: -sum(min(d, side - d) for d in s))
+
+
+def entry_order(at, side):
+    if side != 4:
+        return at[2] < 0, at[2] < 0
+    cost = 0
+    for place, table in zip(at, ((0, 8, 17, 23), (0, 5, 10, 13), (0, 4, 9, 11))):
+        for i in range(1, 4):
+            cost = cost + jnp.where(place == i, table[i], 0)
+    return cost <= 12, cost >= 30
 
 
 def gain_row(ref):
@@ -206,21 +216,47 @@
     for copy in cache_out:
         copy.start()
 
+    early, late = entry_order(at, side)
+    attn_copy = pltpu.make_async_remote_copy(src_ref=as_v, dst_ref=ar_v, send_sem=tp_sem.at[0], recv_sem=tp_sem.at[1],
+                                             device_id={'tp': other}, device_id_type=MESH)
+
+    def project(cols):
+        as_v[:, cols] = jnp.dot(mix_v[...], wo_v[:, cols], preferred_element_type=F32).astype(BF16)
+
+    def finish_projection():
+        project(pl.ds(HALF, HALF))
+        if rest:
+            pltpu.make_async_copy(wd_h.at[pl.ds(half, rest)], wo_v.at[pl.ds(0, rest)], w_sem.at[13]).start()
+        attn_copy.start()
+
+    def middle():
+        attn_copy.wait()
+        mid = (x_v[...].astype(F32) + (as_v[...].astype(F32) + ar_v[...].astype(F32))).astype(BF16)
+        h_v[...] = mid
+        mid = mid.astype(F32)
+        c_v[...] = (mid * inv_rms(mid) * gain_row(gres_v)).astype(BF16)
+
+    def gate_up(i):
+        cols = ff_cols[i]
+        arrive(wg_v.at[:, cols], ff_sem.at[2 * i])
+        arrive(wu_v.at[:, cols], ff_sem.at[2 * i + 1])
+        gate = jnp.dot(c_v[...], wg_v[:, cols], preferred_element_type=F32)
+        up = jnp.dot(c_v[...], wu_v[:, cols], preferred_element_type=F32)
+        act_v[:, cols] = silu_mul(gate, up)
+
+    def gate_up_first():
+        gate_up(0)
+
+    arrive(wo_v, w_sem.at[6])
+    project(pl.ds(0, HALF))
+
     others = pl.ds(0, EP - 1)
     pltpu.make_async_copy(dr_v.at[others], dr_v.at[others], ep_sem.at[1]).wait()
     rows_copy = pltpu.make_async_remote_copy(src_ref=dr_v, dst_ref=dp_v, send_sem=tp_sem.at[4], recv_sem=tp_sem.at[5],
                                              device_id={'tp': other}, device_id_type=MESH)
     rows_copy.start()
 
-    arrive(wo_v, w_sem.at[6])
-
-    as_v[...] = jnp.dot(mix_v[...], wo_v[...], preferred_element_type=F32).astype(BF16)
-    if rest:
-        pltpu.make_async_copy(wd_h.at[pl.ds(half, rest)], wo_v.at[pl.ds(0, rest)], w_sem.at[13]).start()
-    attn_copy = pltpu.make_async_remote_copy(src_ref=as_v, dst_ref=ar_v, send_sem=tp_sem.at[0], recv_sem=tp_sem.at[1],
-                                             device_id={'tp': other}, device_id_type=MESH)
-    attn_copy.start()
-
+    pl.when(jnp.logical_not(late))(finish_projection)
     arrive(eg_v, w_sem.at[7])
     arrive(eu_v, w_sem.at[8])
     near_v[...] = dr_v[...].reshape(slots, HALF + 128)
@@ -247,11 +283,8 @@
                                             device_id={'tp': other}, device_id_type=MESH)
     sum_copy.start()
     own_v[...] = expert_down(mine_half)
-    attn_copy.wait()
-    mid = (x_v[...].astype(F32) + (as_v[...].astype(F32) + ar_v[...].astype(F32))).astype(BF16)
-    h_v[...] = mid
-    mid = mid.astype(F32)
-    c_v[...] = (mid * inv_rms(mid) * gain_row(gres_v)).astype(BF16)
+    pl.when(jnp.logical_not(late))(middle)
+
     arrive(wr_v, w_sem.at[0])
     logits = jnp.dot(m_v[...], wr_v[...], preferred_element_type=F32)
     expd = jnp.exp(logits - jnp.max(logits, axis=-1, keepdims=True))
@@ -263,17 +296,17 @@
     slot_lane = iota((T, slots), 1).astype(F32)
     take = [jnp.where(slot_lane == s, 1.0, 0.0).astype(BF16) for s in slot_cols]
 
+    pl.when(early)(gate_up_first)
     sum_copy.wait()
     rs_v[...] = (own_v[...] + xr_v[...].astype(F32)).astype(BF16).reshape(EP, CAP, HALF)
     exchange(rs_v, rr_v, 2)
     rr_v[me] = rs_v[me]
 
-    for i, cols in enumerate(ff_cols):
-        arrive(wg_v.at[:, cols], ff_sem.at[2 * i])
-        arrive(wu_v.at[:, cols], ff_sem.at[2 * i + 1])
-        gate = jnp.dot(c_v[...], wg_v[:, cols], preferred_element_type=F32)
-        up = jnp.dot(c_v[...], wu_v[:, cols], preferred_element_type=F32)
-        act_v[:, cols] = silu_mul(gate, up)
+    pl.when(late)(finish_projection)
+    pl.when(late)(middle)
+    pl.when(jnp.logical_not(early))(gate_up_first)
+    for i in range(1, blocks):
+        gate_up(i)
 
     arrive(wq_v.at[pl.ds(0, half)], w_sem.at[12])
     if rest:

time: 33.4 us -> 33.6 us (level)
  no operation moved by 1% of the time
where the time goes in v7:
time: 33.6 us; the launch traced here: 33.4 us
  Pallas kernels  32.6 us (97%)
  between operations  0.81 us (2%)
    pallas_call x1, Pallas kernels, local_layer(): pl.pallas_call(functools.partial(layer_kernel, dims), out_shape=(jax.Shap...  30.5 us
    pallas_call x1, Pallas kernels, settle(): pl.pallas_call(settle_kernel, out_shape=tuple((jax.ShapeDtypeStruct(s, BF...  2.1 us

profile of v7, /device:TPU:1, one launch (start us, length us, event | category | flops | bytes accessed | tf_op | source)
XLA Modules:
  0.0 33.4 jit_solution(15170562915343040486)
XLA Ops:
  0.6 30.5 %layer.1 = (bf16[2,32,1024]{2,1,0:T(8,128)(2,1)}, bf16[2048,128]{1,0:T(8,128)(2,1)}, bf16[2048,128]{1,0:T(8,128)(2,1)}) custom-call(bf16[32,2048]{1,0:T(8,128)(2,1)} %x_h.1, s32[1,32]{1,0:T(1,128)} %bitcast.15, s32[2,32]{1,0:T(2,128)} %bitcast.14, bf16[2048,128]{1,0:T(8,128)(2,1)} %bitcast.9, bf16[2048,128]{1,0:T(8,128)(2,1)} %bitcast.10, ...), custom_call_target="tpu_custom_call" | custom-call | tf_op jit(solution)/shard_map/layer/pallas_call | solution.py:418
  31.2 2.1 %settle.1 = (bf16[32,2048]{1,0:T(8,128)(2,1)}, bf16[2048,128]{1,0:T(8,128)(2,1)}, bf16[2048,128]{1,0:T(8,128)(2,1)}) custom-call(bf16[2,32,1024]{2,1,0:T(8,128)(2,1)} %get-tuple-element.9.half_h, bf16[2048,128]{1,0:T(8,128)(2,1)} %get-tuple-element.10.ki_h, bf16[2048,128]{1,0:T(8,128)(2,1)} %get-tuple-element.11.vi_h), custom_call_target="tpu_custom_call" | custom-call | tf_op jit(solution)/shard_map/settle/pallas_call | solution.py:369

commit v8 on v7

--- a/solution.py
+++ b/solution.py
@@ -96,7 +96,7 @@
     for i, (src, dst) in enumerate(small):
         pltpu.make_async_copy(src, dst, small_sem.at[i]).wait()
 
-    fetch(wq_h, wq_v, w_sem.at[3], 2)
+    fetch(wq_h, wq_v, w_sem.at[3], 1)
 
     wide = x_v[...].astype(F32)
     scaled = wide * inv_rms(wide)
@@ -148,7 +148,19 @@
 
     fetch(kc_h, kc_v, w_sem.at[4], 1)
     fetch(vc_h, vc_v, w_sem.at[5], 1)
-    fetch(wo_h, wo_v, w_sem.at[6], 2)
+    fetch(wo_h, wo_v, w_sem.at[6], 1)
+    fetch(eg_h, eg_v, w_sem.at[7], 1)
+    fetch(eu_h, eu_v, w_sem.at[8], 1)
+    fetch(ed_h, ed_v, w_sem.at[9], 1)
+    blocks = 3 if F % (3 * TILE) == 0 else 1
+    ff_cols = [pl.ds(i * (F // blocks), F // blocks) for i in range(blocks)]
+
+    def fetch_gate_up(i):
+        for w, (src, dst) in enumerate(((wg_h, wg_v), (wu_h, wu_v))):
+            pltpu.make_async_copy(src.at[:, ff_cols[i]], dst.at[:, ff_cols[i]], ff_sem.at[2 * i + w]).start()
+
+    for i in range(min(2, blocks)):
+        fetch_gate_up(i)
 
     pl.semaphore_wait(barrier, EP)
 
@@ -159,19 +171,13 @@
 
     exchange(ds_v, dr_v, 0)
     dr_v[me] = ds_v[me]
-    fetch(eg_h, eg_v, w_sem.at[7], 1)
-    fetch(eu_h, eu_v, w_sem.at[8], 1)
-    fetch(ed_h, ed_v, w_sem.at[9], 1)
+
+    arrive(wq_v, w_sem.at[3])
+    for i in range(2, blocks):
+        fetch_gate_up(i)
     fetch(wr_h, wr_v, w_sem.at[0], 1)
 
-    arrive(wq_v, w_sem.at[3])
-
     q_v[...] = jnp.dot(a_v[...], wq_v[...], preferred_element_type=F32)
-    blocks = 3 if F % (3 * TILE) == 0 else 1
-    ff_cols = [pl.ds(i * (F // blocks), F // blocks) for i in range(blocks)]
-    for i, cols in enumerate(ff_cols):
-        pltpu.make_async_copy(wg_h.at[:, cols], wg_v.at[:, cols], ff_sem.at[2 * i]).start()
-        pltpu.make_async_copy(wu_h.at[:, cols], wu_v.at[:, cols], ff_sem.at[2 * i + 1]).start()
     half = min(wd_h.shape[0], wq_v.shape[0])
     rest = wd_h.shape[0] - half
     pltpu.make_async_copy(wd_h.at[pl.ds(0, half)], wq_v.at[pl.ds(0, half)], w_sem.at[12]).start()

time: 33.6 us -> 34.7 us (1.033)
  Pallas kernels: 32.6 us -> 33.7 us
    pallas_call x1, Pallas kernels: 30.5 us -> 31.6 us  [local_layer(): pl.pallas_call(functools.partial(layer_kernel, dims), out_shape=(jax.Shap...]
where the time goes in v8:
time: 34.7 us; the launch traced here: 34.5 us
  Pallas kernels  33.7 us (97%)
  between operations  0.81 us (2%)
    pallas_call x1, Pallas kernels, local_layer(): pl.pallas_call(functools.partial(layer_kernel, dims), out_shape=(jax.Shap...  31.6 us
    pallas_call x1, Pallas kernels, settle(): pl.pallas_call(settle_kernel, out_shape=tuple((jax.ShapeDtypeStruct(s, BF...  2.1 us

profile of v8, /device:TPU:1, one launch (start us, length us, event | category | flops | bytes accessed | tf_op | source)
XLA Modules:
  0.0 34.5 jit_solution(10829770942087057452)
XLA Ops:
  0.6 31.6 %layer.1 = (bf16[2,32,1024]{2,1,0:T(8,128)(2,1)}, bf16[2048,128]{1,0:T(8,128)(2,1)}, bf16[2048,128]{1,0:T(8,128)(2,1)}) custom-call(bf16[32,2048]{1,0:T(8,128)(2,1)} %x_h.1, s32[1,32]{1,0:T(1,128)} %bitcast.15, s32[2,32]{1,0:T(2,128)} %bitcast.14, bf16[2048,128]{1,0:T(8,128)(2,1)} %bitcast.9, bf16[2048,128]{1,0:T(8,128)(2,1)} %bitcast.10, ...), custom_call_target="tpu_custom_call" | custom-call | tf_op jit(solution)/shard_map/layer/pallas_call | solution.py:424
  32.3 2.1 %settle.1 = (bf16[32,2048]{1,0:T(8,128)(2,1)}, bf16[2048,128]{1,0:T(8,128)(2,1)}, bf16[2048,128]{1,0:T(8,128)(2,1)}) custom-call(bf16[2,32,1024]{2,1,0:T(8,128)(2,1)} %get-tuple-element.9.half_h, bf16[2048,128]{1,0:T(8,128)(2,1)} %get-tuple-element.10.ki_h, bf16[2048,128]{1,0:T(8,128)(2,1)} %get-tuple-element.11.vi_h), custom_call_target="tpu_custom_call" | custom-call | tf_op jit(solution)/shard_map/settle/pallas_call | solution.py:375

commit v9 on v7

--- a/solution.py
+++ b/solution.py
@@ -150,6 +150,22 @@
     fetch(vc_h, vc_v, w_sem.at[5], 1)
     fetch(wo_h, wo_v, w_sem.at[6], 2)
 
+    early, late = entry_order(at, side)
+    blocks = 3 if F % (3 * TILE) == 0 else 1
+    ff_cols = [pl.ds(i * (F // blocks), F // blocks) for i in range(blocks)]
+
+    def stream_ahead():
+        arrive(wq_v, w_sem.at[3])
+        fetch(eg_h, eg_v, w_sem.at[7], 1)
+        fetch(eu_h, eu_v, w_sem.at[8], 1)
+        fetch(ed_h, ed_v, w_sem.at[9], 1)
+        fetch(wr_h, wr_v, w_sem.at[0], 1)
+        for i, cols in enumerate(ff_cols):
+            pltpu.make_async_copy(wg_h.at[:, cols], wg_v.at[:, cols], ff_sem.at[2 * i]).start()
+            pltpu.make_async_copy(wu_h.at[:, cols], wu_v.at[:, cols], ff_sem.at[2 * i + 1]).start()
+
+    pl.when(jnp.logical_not(late))(stream_ahead)
+
     pl.semaphore_wait(barrier, EP)
 
     def exchange(src, dst, sem):
@@ -159,19 +175,10 @@
 
     exchange(ds_v, dr_v, 0)
     dr_v[me] = ds_v[me]
-    fetch(eg_h, eg_v, w_sem.at[7], 1)
-    fetch(eu_h, eu_v, w_sem.at[8], 1)
-    fetch(ed_h, ed_v, w_sem.at[9], 1)
-    fetch(wr_h, wr_v, w_sem.at[0], 1)
-
-    arrive(wq_v, w_sem.at[3])
+    pl.when(late)(stream_ahead)
+
 
     q_v[...] = jnp.dot(a_v[...], wq_v[...], preferred_element_type=F32)
-    blocks = 3 if F % (3 * TILE) == 0 else 1
-    ff_cols = [pl.ds(i * (F // blocks), F // blocks) for i in range(blocks)]
-    for i, cols in enumerate(ff_cols):
-        pltpu.make_async_copy(wg_h.at[:, cols], wg_v.at[:, cols], ff_sem.at[2 * i]).start()
-        pltpu.make_async_copy(wu_h.at[:, cols], wu_v.at[:, cols], ff_sem.at[2 * i + 1]).start()
     half = min(wd_h.shape[0], wq_v.shape[0])
     rest = wd_h.shape[0] - half
     pltpu.make_async_copy(wd_h.at[pl.ds(0, half)], wq_v.at[pl.ds(0, half)], w_sem.at[12]).start()
@@ -216,7 +223,6 @@
     for copy in cache_out:
         copy.start()
 
-    early, late = entry_order(at, side)
     attn_copy = pltpu.make_async_remote_copy(src_ref=as_v, dst_ref=ar_v, send_sem=tp_sem.at[0], recv_sem=tp_sem.at[1],
                                              device_id={'tp': other}, device_id_type=MESH)
 

time: 33.6 us -> 34.9 us (1.039)
  Pallas kernels: 32.6 us -> 33.9 us
    pallas_call x1, Pallas kernels: 30.5 us -> 31.8 us  [local_layer(): pl.pallas_call(functools.partial(layer_kernel, dims), out_shape=(jax.Shap...]
where the time goes in v9:
time: 34.9 us; the launch traced here: 34.7 us
  Pallas kernels  33.9 us (97%)
  between operations  0.81 us (2%)
    pallas_call x1, Pallas kernels, local_layer(): pl.pallas_call(functools.partial(layer_kernel, dims), out_shape=(jax.Shap...  31.8 us
    pallas_call x1, Pallas kernels, settle(): pl.pallas_call(settle_kernel, out_shape=tuple((jax.ShapeDtypeStruct(s, BF...  2.1 us

profile of v9, /device:TPU:1, one launch (start us, length us, event | category | flops | bytes accessed | tf_op | source)
XLA Modules:
  0.0 34.7 jit_solution(4412195240297822556)
XLA Ops:
  0.6 31.8 %layer.1 = (bf16[2,32,1024]{2,1,0:T(8,128)(2,1)}, bf16[2048,128]{1,0:T(8,128)(2,1)}, bf16[2048,128]{1,0:T(8,128)(2,1)}) custom-call(bf16[32,2048]{1,0:T(8,128)(2,1)} %x_h.1, s32[1,32]{1,0:T(1,128)} %bitcast.15, s32[2,32]{1,0:T(2,128)} %bitcast.14, bf16[2048,128]{1,0:T(8,128)(2,1)} %bitcast.9, bf16[2048,128]{1,0:T(8,128)(2,1)} %bitcast.10, ...), custom_call_target="tpu_custom_call" | custom-call | tf_op jit(solution)/shard_map/layer/pallas_call | solution.py:424
  32.5 2.1 %settle.1 = (bf16[32,2048]{1,0:T(8,128)(2,1)}, bf16[2048,128]{1,0:T(8,128)(2,1)}, bf16[2048,128]{1,0:T(8,128)(2,1)}) custom-call(bf16[2,32,1024]{2,1,0:T(8,128)(2,1)} %get-tuple-element.9.half_h, bf16[2048,128]{1,0:T(8,128)(2,1)} %get-tuple-element.10.ki_h, bf16[2048,128]{1,0:T(8,128)(2,1)} %get-tuple-element.11.vi_h), custom_call_target="tpu_custom_call" | custom-call | tf_op jit(solution)/shard_map/settle/pallas_call | solution.py:375
